TPU v7x, 512 devices: a whole 4x8x8 slice. The times are simulated.
512 devices in a mesh: seq: 64 (over z, y_hi, x), tp: 8 (over y_lo, core).
Axes of the slice: x: 4, y: 8 (y_hi: 2, y_lo: 4; y = y_hi * 4 + y_lo), z: 8, core: 2. Of those that a mesh axis runs over, the one named last changes fastest.
Arguments:
- tokens: bfloat16 [8192, 2048], P('seq', 'tp'), may hold values from -6 to 6
- ln_gain: bfloat16 [2048], replicated, may hold values from 0.5 to 4.1
- w_qkv: bfloat16 [3, 2048, 2048], P(None, None, 'tp'), may hold values from -0.15467961 to 0.15467961
- w_out: bfloat16 [2048, 2048], P('tp'), may hold values from -0.1875 to 0.1875
Outputs:
- mixed: bfloat16 [8192, 2048], P('seq', 'tp')
All inputs are finite; a program needn't handle non-finite values.
Results may differ from a plain program's by a relative error of at most 0.011.
Values may be sent and summed in bfloat16 or wider, within the bound.
No kernel may reach another device: no remote copies, remote signals or barrier semaphores. Data moves between devices by JAX's collectives and lax.ppermute only.
A program may use at most 64 MiB of HBM per device.

v0:
```python
import jax
import jax.numpy as jnp
from jax import lax
from jax.sharding import Mesh
from jax.sharding import PartitionSpec as P

HEAD_DIM = 128
TP = ("tp_0", "tp_1")


def joined_along(tiles, dim):
    lengths = list(tiles.shape[1:])
    lengths[dim] *= tiles.shape[0]
    return jnp.moveaxis(tiles, 0, dim).reshape(lengths)


def all_blocks(shard, axes, turns):
    tiles = shard[None]
    for k in turns:
        tiles = lax.all_gather(tiles, axes[k], axis=0, tiled=True)
    held = [lax.axis_size(axes[k]) for k in reversed(turns)]
    tiles = tiles.reshape(*held, *shard.shape)
    turned = sorted(range(len(turns)), key=lambda place: turns[len(turns) - 1 - place])
    return tiles.transpose(*turned, *range(len(turns), tiles.ndim)).reshape(-1, *shard.shape)


def gathered_by_axis(shard, axes, turns, dim):
    return joined_along(all_blocks(shard, axes, turns), dim)


def split_up(shard, dim, devices):
    before, after = (shard.shape[:dim], shard.shape[dim + 1 :])
    return jnp.moveaxis(shard.reshape(*before, devices, -1, *after), dim, 0)


def summed_on_arrival(shard, axis, dim):
    devices = lax.axis_size(axis)
    tiles = lax.all_to_all(split_up(shard, dim, devices), axis, 0, 0, tiled=True)
    return jnp.sum(tiles.astype(jnp.float32), axis=0)


def attend_block(totals, queries, block_kv, factor):
    running, denoms, accum = totals
    heads_here = queries.shape[1]
    keys_part = block_kv[0].reshape(block_kv.shape[1], heads_here, queries.shape[2])
    vals_part = block_kv[1].reshape(block_kv.shape[1], heads_here, queries.shape[2])
    scores = (
        jnp.einsum("thc,shc->ths", queries, keys_part, preferred_element_type=jnp.float32) * factor
    )
    highest = jnp.maximum(running, jnp.max(scores, axis=2))
    expon = jnp.exp(scores - highest[:, :, None])
    denoms = jnp.sum(expon, axis=2)
    weights = expon.astype(jnp.bfloat16)
    accum = jnp.einsum("ths,shc->thc", weights, vals_part, preferred_element_type=jnp.float32)
    return (highest, denoms, accum)


def start_totals(rows, heads_count):
    return (
        jnp.full((rows, heads_count), -1e30, jnp.float32),
        jnp.zeros((rows, heads_count), jnp.float32),
        jnp.zeros((rows, heads_count, HEAD_DIM), jnp.float32),
    )


def on_device(tokens, ln_gain, w_qkv, w_out):
    tok_rows = tokens.shape[0]
    whole = gathered_by_axis(tokens, TP, (0, 1), 1)
    values = whole.astype(jnp.float32)
    average = jnp.mean(values, axis=1, keepdims=True)
    second = jnp.mean(values * values, axis=1, keepdims=True)
    normed = (
        (values - average)
        * lax.rsqrt(second - average * average + 1e-06)
        * ln_gain.astype(jnp.float32)
    ).astype(jnp.bfloat16)
    projected = jnp.einsum("td,jdc->jtc", normed, w_qkv, preferred_element_type=jnp.float32).astype(
        jnp.bfloat16
    )
    heads_here = w_qkv.shape[2] // HEAD_DIM
    factor = HEAD_DIM ** (-0.5)
    queries = projected[0].reshape(tok_rows, heads_here, HEAD_DIM)
    keys_vals = projected[1:3]
    initial = start_totals(tok_rows, heads_here)
    final = attend_block(
        initial, queries, lax.all_gather(keys_vals, "seq", axis=1, tiled=True), factor
    )
    context = (
        (final[2] / final[1][:, :, None])
        .reshape(tok_rows, heads_here * HEAD_DIM)
        .astype(jnp.bfloat16)
    )
    summed = summed_on_arrival(
        lax.dot_general(
            w_out, context, (((0,), (1,)), ((), ())), preferred_element_type=jnp.float32
        ).astype(jnp.bfloat16),
        TP,
        0,
    )
    return (tokens.astype(jnp.float32) + summed.T).astype(jnp.bfloat16)


def solution(mesh):
    split = Mesh(mesh.devices.reshape(mesh.shape["seq"], 4, 2), ("seq", "tp_0", "tp_1"))
    placed = (P("seq", TP), P(), P(None, None, TP), P(TP, None))
    return jax.shard_map(
        on_device, mesh=split, in_specs=placed, out_specs=P("seq", TP), check_vma=False
    )
```

profile of v0, /device:TPU:1, one launch (start us, length us, event | category | flops | bytes accessed | tf_op | source)
XLA Modules:
  0.0 287.6 jit_solution(10540969496366223831)
XLA Ops:
  6.5 12.4 %all-gather = bf16[512,256]{1,0:T(8,128)(2,1)S(1)} all-gather(bf16[128,256]{1,0:T(8,128)(2,1)} %param.4), channel_id=2, replica_groups=mesh['seq'=64,'tp_0'=4,'tp_1'=2] {'tp_0'}, dimensions={0}, use_global_device_ids=true | all-gather | bytes 327680 | tf_op jit(solution)/shard_map/all_gather | solution.py:20
  18.9 10.5 %all_gather.10 = bf16[8,128,256]{2,1,0:T(8,128)(2,1)S(1)} all-gather(bf16[4,128,256]{2,1,0:T(8,128)(2,1)S(1)} %bitcast.49), channel_id=1, replica_groups=mesh['seq'=64,'tp_0'=4,'tp_1'=2] {'tp_1'}, dimensions={0}, use_global_device_ids=true | all-gather | bytes 786432 | tf_op jit(solution)/shard_map/all_gather | solution.py:20
  29.4 0.2 convert_reduce_fusion.1
  29.5 0.1 convert_element_type.84
  29.6 0.7 convert_element_type.68
  30.3 0.2 multiply_reduce_fusion
  30.5 1.1 copy.20
  31.6 2.6 copy.21
  34.2 1.6 fusion.19
  35.7 0.6 fusion.7
  36.4 0.7 slice.16
  37.0 0.0 all-gather.3.cloned.1.call-update
  37.1 176.1 %all-gather.3.cloned.1.call-done = bf16[2,8192,256]{2,1,0:T(8,128)(2,1)} async-done(((bf16[2,128,256]{2,1,0:T(8,128)(2,1)}), bf16[2,8192,256]{2,1,0:T(8,128)(2,1)}) %all-gather.3.cloned.1.call-update) | async-done | bytes 8388624 | tf_op jit(solution)/shard_map/all_gather | solution.py:86
  213.2 5.7 %fusion.23 = (bf16[1,8192,256]{2,1,0:T(8,128)(2,1)}, bf16[1,8192,256]{2,1,0:T(8,128)(2,1)}) fusion(bf16[2,8192,256]{2,1,0:T(8,128)(2,1)} %all-gather.3.cloned.1.call-done), kind=kLoop, calls=%fused_computation.29 | loop fusion | bytes 16777216 | tf_op jit(solution)/shard_map/slice | solution.py:45
  218.9 6.9 %reshape_squeeze.10 = bf16[8192,2,128]{2,1,0:T(2,128)(2,1)} reshape(bf16[1,8192,256]{2,1,0:T(8,128)(2,1)} %get-tuple-element.5) | data formatting | bytes 8388608 | tf_op jit(solution)/shard_map/reshape;squeeze | solution.py:45
  225.9 6.7 %fusion.24 = (f32[128,2]{0,1:T(2,128)S(1)}, f32[128,2,8192]{0,2,1:T(8,128)}) fusion(bf16[128,2,128]{2,1,0:T(2,128)(2,1)S(1)} %reshape_squeeze.11, bf16[8192,2,128]{2,1,0:T(2,128)(2,1)} %reshape_squeeze.10), kind=kOutput, calls=%fused_computation.30 | convolution fusion | flops 541064960 | bytes 12649472 | tf_op jit(solution)/shard_map/thc,shc->ths/dot_general | solution.py:48
  232.5 6.4 %copy.31 = bf16[1,8192,256]{1,2,0:T(8,128)(2,1)} copy(bf16[1,8192,256]{2,1,0:T(8,128)(2,1)} %get-tuple-element.6) | data formatting | bytes 8388608 | tf_op jit(solution)/shard_map/reshape;squeeze | solution.py:46
  238.9 4.6 %fusion.1 = f32[128,2]{0,1:T(2,128)S(1)} fusion(f32[128,2,8192]{0,2,1:T(8,128)} %get-tuple-element.10, f32[128,2]{0,1:T(2,128)S(1)} %broadcast_maximum_fusion), kind=kLoop, calls=%fused_computation.3 | loop fusion | flops 4194048 | bytes 8390656 | tf_op jit(solution)/shard_map/reduce_sum | solution.py:52
  243.5 1.1 copy-done.1
  244.7 4.2 %fusion.14 = bf16[128,2,128]{0,2,1:T(8,128)(2,1)S(1)} fusion(bf16[8192,2,128]{0,2,1:T(8,128)(2,1)} %bitcast.43, f32[128,2,8192]{0,2,1:T(8,128)S(1)} %copy-done.1, f32[128,2]{0,1:T(2,128)S(1)} %broadcast_maximum_fusion, f32[128,2]{0,1:T(2,128)S(1)} %fusion.1), kind=kOutput, calls=%fused_computation.13 | convolution fusion | flops 541130752 | bytes 12650496 | tf_op jit(solution)/shard_map/ths,shc->thc/dot_general | solution.py:54
  248.9 0.3 convolution_convert_fusion
  249.3 30.7 %all_to_all.5 = bf16[8,256,128]{1,2,0:T(8,128)(2,1)S(1)} all-to-all(bf16[8,256,128]{1,2,0:T(8,128)(2,1)S(1)} %bitcast.48), channel_id=1, replica_groups=mesh['seq'=64,'tp_0'=4,'tp_1'=2] {'tp_0','tp_1'}, dimensions={0} | all-to-all | bytes 1048576 | tf_op jit(solution)/shard_map/all_to_all | solution.py:38
  280.0 0.1 convert_reduce_fusion
  280.1 0.6 fusion.21
  (13 shorter events, 0.1 us)
Async XLA Ops:
  6.5 29.2 %copy-start = (bf16[3,2048,256]{2,1,0:T(8,128)(2,1)S(1)}, bf16[3,2048,256]{2,1,0:T(8,128)(2,1)}, u32[]{:S(2)}) copy-start(bf16[3,2048,256]{2,1,0:T(8,128)(2,1)} %param.6) | copy-start | bytes 9437188
  6.5 206.7 %all-gather.3.cloned.1.call-start = ((), (), s32[]{:S(2)}) async-start(), calls=%async_computation.1 | async-start | bytes 8519680 | tf_op jit(solution)/shard_map/all_gather | solution.py:86
  238.9 5.8 %copy-start.1 = (f32[128,2,8192]{0,2,1:T(8,128)S(1)}, f32[128,2,8192]{0,2,1:T(8,128)}, u32[]{:S(2)}) copy-start(f32[128,2,8192]{0,2,1:T(8,128)} %get-tuple-element.10) | copy-start | bytes 25165828
  244.7 4.2 %copy-start.2 = (bf16[256,2048]{1,0:T(8,128)(2,1)S(1)}, bf16[256,2048]{1,0:T(8,128)(2,1)}, u32[]{:S(2)}) copy-start(bf16[256,2048]{1,0:T(8,128)(2,1)} %param.7) | copy-start | bytes 3145732
  248.9 31.2 %copy-start.3 = (bf16[128,256]{1,0:T(8,128)(2,1)S(1)}, bf16[128,256]{1,0:T(8,128)(2,1)}, u32[]{:S(2)}) copy-start(bf16[128,256]{1,0:T(8,128)(2,1)} %param.4) | copy-start | bytes 196612
Sparse Core Ops, SparseCore 0:
  37.2 175.9 all-gather.2
where the time goes:
time: 288 us
  waiting for transfers between devices  176 us (61%)
  blocking collectives  53.6 us (19%)
  local copies, waits for them, and re-layouts  24.6 us (9%)
  between operations  13.5 us (5%)
  matrix products  11.8 us (4%)
  other arithmetic  8.01 us (3%)
    all_gather x1, waiting for transfers between devices, on_device(): lax.all_gather(keys_vals, 'seq', axis=1, tiled=True)  176 us
    all_to_all x1, blocking collectives, summed_on_arrival(): lax.all_to_all(split_up(shard, dim, devices), axis, 0, 0, tiled=True)  30.7 us
    all_gather x2, blocking collectives, all_blocks(): tiles = lax.all_gather(tiles, axes[k], axis=0, tiled=True)  22.8 us
    another operation x1, local copies, waits for them, and re-layouts, attend_block(): block_kv[0].reshape(block_kv.shape[1], heads_here, queries.shape[2])  6.93 us
    dot_general x1, matrix products, attend_block(): jnp.einsum('thc,shc->ths', queries, keys_part, preferred_element_type=jnp...  6.67 us
    another operation x1, local copies, waits for them, and re-layouts, attend_block(): block_kv[1].reshape(block_kv.shape[1], heads_here, queries.shape[2])  6.37 us
  transfers between devices with their start and end apart: 1, of which 1 were waited for; matrix products, arithmetic and copies ran while one was open for 0% of the time, Pallas kernels for 0%

commit v1 on v0

v1 whole, which is shorter than its diff:
```python
import functools
import math

import jax
import jax.numpy as jnp
from jax import lax
from jax.experimental import pallas as pl
from jax.experimental.pallas import tpu as pltpu
from jax.sharding import Mesh
from jax.sharding import PartitionSpec as P

HEAD_DIM = 128
ROWS = 128
GROUP = 8
STAT_ROWS = 8
LOG2E = math.log2(math.e)
bf16 = jnp.bfloat16
f32 = jnp.float32


def vmem(count):
    return [pl.BlockSpec(memory_space=pltpu.VMEM)] * count


def norm_project(x_ref, gain_ref, w_ref, q_ref, kv_ref):
    width = x_ref.shape[3]
    blocks = [(y, c) for y in range(4) for c in range(2)]
    total = jnp.zeros((ROWS, width), f32)
    squares = jnp.zeros((ROWS, width), f32)
    for y, c in blocks:
        part = x_ref[c, y].astype(f32)
        total += part
        squares += part * part
    features = width * len(blocks)
    average = jnp.sum(total, axis=1, keepdims=True) / features
    second = jnp.sum(squares, axis=1, keepdims=True) / features
    inverse = lax.rsqrt(second - average * average + 1e-6)
    sums = [jnp.zeros((ROWS, width), f32) for _ in range(3)]
    for t, (y, c) in enumerate(blocks):
        part = x_ref[c, y].astype(f32)
        gain = gain_ref[t : t + 1, :].astype(f32)
        normed = ((part - average) * inverse * gain).astype(bf16)
        for j in range(3):
            sums[j] += jnp.dot(
                normed, w_ref[j, t * width : (t + 1) * width, :], preferred_element_type=f32
            )
    query = sums[0].astype(bf16)
    key = sums[1].astype(bf16)
    value = sums[2]
    turned = jnp.concatenate(
        [value[:, h * HEAD_DIM : (h + 1) * HEAD_DIM].T for h in range(2)], axis=1
    ).astype(bf16)
    for i in range(GROUP):
        q_ref[i] = query
        kv_ref[i, :, : 2 * HEAD_DIM] = key
        kv_ref[i, :, 2 * HEAD_DIM :] = turned


def attend(q_ref, kv_ref, o_ref):
    factor = HEAD_DIM**-0.5 * LOG2E
    for h in range(2):
        cols = slice(h * HEAD_DIM, (h + 1) * HEAD_DIM)
        vcols = slice((2 + h) * HEAD_DIM, (3 + h) * HEAD_DIM)
        keys = kv_ref[:, :, cols].reshape(GROUP * ROWS, HEAD_DIM)
        values = jnp.concatenate([kv_ref[s, :, vcols] for s in range(GROUP)], axis=1)
        for pair in range(GROUP // 2):
            query = q_ref[2 * pair : 2 * pair + 2, :, cols].reshape(2 * ROWS, HEAD_DIM)
            scores = lax.dot_general(
                keys, query, (((1,), (1,)), ((), ())), preferred_element_type=f32
            )
            highest = jnp.max(scores, axis=0, keepdims=True)
            expon = jnp.exp2((scores - highest) * factor)
            denom = jnp.sum(expon, axis=0, keepdims=True)
            context = jnp.dot(values, expon.astype(bf16), preferred_element_type=f32)
            context = (context / denom).astype(bf16)
            level = highest * factor + jnp.log2(denom)
            first = level.astype(bf16).astype(f32)
            middle = (level - first).astype(bf16).astype(f32)
            last = level - first - middle
            stats = jnp.concatenate(
                [first, middle, last, jnp.zeros((STAT_ROWS - 3, 2 * ROWS), f32)], axis=0
            ).astype(bf16)
            for i in range(2):
                span = slice(i * ROWS, (i + 1) * ROWS)
                o_ref[2 * pair + i, :HEAD_DIM, cols] = context[:, span]
                o_ref[2 * pair + i, HEAD_DIM:, cols] = stats[:, span]


def combine(o_ref, c_ref):
    levels = []
    for s in range(GROUP):
        stats = o_ref[s, HEAD_DIM:, :].astype(f32)
        levels.append(stats[0:1] + stats[1:2] + stats[2:3])
    highest = functools.reduce(jnp.maximum, levels)
    shares = [jnp.exp2(level - highest) for level in levels]
    denom = functools.reduce(jnp.add, shares)
    total = jnp.zeros((HEAD_DIM, 2 * ROWS), f32)
    for s in range(GROUP):
        total += o_ref[s, :HEAD_DIM, :].astype(f32) * (shares[s] / denom)
    c_ref[...] = total.astype(bf16)


def project(own_ref, other_ref, w_ref, w_other_ref, out_ref):
    core = lax.axis_index("core")
    for y in range(4):
        cols = pl.ds(pl.multiple_of((2 * y + core) * 256, 256), 256)
        total = jnp.zeros((ROWS, 256), f32)
        for ctx, w in ((own_ref, w_ref), (other_ref, w_other_ref)):
            for h in range(2):
                total += lax.dot_general(
                    ctx[:, h * ROWS : (h + 1) * ROWS],
                    w[h * HEAD_DIM : (h + 1) * HEAD_DIM, cols],
                    (((0,), (0,)), ((), ())),
                    preferred_element_type=f32,
                )
        out_ref[y] = total.astype(bf16)


def spread(block, count):
    return jnp.broadcast_to(block[None], (count, *block.shape))


def exchange(blocks, axes):
    return lax.all_to_all(blocks, axes, 0, 0, tiled=True)


SWAP = ((0, 1), (1, 0))


def on_device(tokens, ln_gain, w_qkv, w_out):
    shape = jax.ShapeDtypeStruct
    across = exchange(spread(tokens, 4), "y_lo")
    w_other = lax.ppermute(w_out, "core", SWAP)
    whole = lax.all_gather(across, "core", axis=0)
    q_blocks, kv_blocks = pl.pallas_call(
        norm_project,
        out_shape=(shape((GROUP, ROWS, 256), bf16), shape((GROUP, ROWS, 512), bf16)),
        in_specs=vmem(3),
        out_specs=tuple(vmem(2)),
        cost_estimate=pl.CostEstimate(
            flops=2 * ROWS * 2048 * 768, bytes_accessed=5 << 20, transcendentals=0
        ),
    )(whole, ln_gain.reshape(8, 256), w_qkv)
    kv_here = exchange(kv_blocks, ("y_hi", "x"))
    q_here = exchange(q_blocks, "z")
    partial = pl.pallas_call(
        attend,
        out_shape=shape((GROUP, HEAD_DIM + STAT_ROWS, 2 * ROWS), bf16),
        in_specs=vmem(2),
        out_specs=vmem(1)[0],
        compiler_params=pltpu.CompilerParams(vmem_limit_bytes=40 << 20),
        cost_estimate=pl.CostEstimate(
            flops=4 * 1024 * 1024 * 256, bytes_accessed=3 << 20, transcendentals=2 << 20
        ),
    )(q_here, kv_here)
    shares = exchange(partial, "z")
    context = pl.pallas_call(
        combine,
        out_shape=shape((HEAD_DIM, 2 * ROWS), bf16),
        in_specs=vmem(1),
        out_specs=vmem(1)[0],
    )(shares)
    other = lax.ppermute(context, "core", SWAP)
    projected = pl.pallas_call(
        project,
        out_shape=shape((4, ROWS, 256), bf16),
        in_specs=vmem(4),
        out_specs=vmem(1)[0],
    )(context, other, w_out, w_other)
    summed = jnp.sum(exchange(projected, "y_lo").astype(f32), axis=0)
    return (tokens.astype(f32) + summed).astype(bf16)


def solution(mesh):
    grid = Mesh(mesh.devices.reshape(8, 2, 4, 4, 2), ("z", "y_hi", "x", "y_lo", "core"))
    seq, tp = ("z", "y_hi", "x"), ("y_lo", "core")
    return jax.shard_map(
        on_device,
        mesh=grid,
        in_specs=(P(seq, tp), P(), P(None, None, tp), P(tp, None)),
        out_specs=P(seq, tp),
        check_vma=False,
    )
```

time: 288 us -> 132 us (0.46)
  waiting for transfers between devices: 176 us -> 25.8 us
  starting transfers between devices: 0.01 us -> 24.9 us
  local copies, waits for them, and re-layouts: 24.6 us -> 3.47 us
  Pallas kernels: 0 us -> 14.1 us
  between operations: 13.5 us -> 0.06 us
  matrix products: 11.8 us -> 0 us
  other arithmetic: 8.01 us -> 0.68 us
  blocking collectives: 53.6 us -> 60.9 us
    all_gather x1 -> x0, waiting for transfers between devices: 176 us -> none  [on_device(): lax.all_gather(keys_vals, 'seq', axis=1, tiled=True)]
    all_to_all x0 -> x2, waiting for transfers between devices: none -> 24.8 us  [exchange(): return lax.all_to_all(blocks, axes, 0, 0, tiled=True)]
    all_to_all x1 -> x3, blocking collectives: 30.7 us -> 53 us  [exchange(): return lax.all_to_all(blocks, axes, 0, 0, tiled=True)]
    all_gather x2 -> x1, blocking collectives: 22.8 us -> 7.88 us  [on_device(): whole = lax.all_gather(across, 'core', axis=0)]
    pallas_call x0 -> x4, Pallas kernels: none -> 14.1 us  [the longest x1 5.47 us: on_device(): pl.pallas_call(attend, out_shape=shape((GROUP, HEAD_DIM + STAT_ROWS, 2 *...]
    all_to_all x0 -> x2, starting transfers between devices: none -> 13.5 us  [exchange(): return lax.all_to_all(blocks, axes, 0, 0, tiled=True)]
    another operation x3 -> x0, local copies, waits for them, and re-layouts: 13.3 us -> none  [the longest x1 6.93 us: attend_block(): block_kv[0].reshape(block_kv.shape[1], heads_here, queries.shape[2])]
    dot_general x4 -> x0, matrix products: 11.8 us -> none  [the longest x1 6.67 us: attend_block(): jnp.einsum('thc,shc->ths', queries, keys_part, preferred_element_type=jnp...]
  transfers between devices with their start and end apart: 1 -> 4, of which waited for: 1 -> 3; matrix products, arithmetic and copies ran while one was open for 0% -> 1% of each run, Pallas kernels for 0% -> 6%
where the time goes in v1:
time: 132 us; the launch traced here: 130 us
  blocking collectives  60.9 us (46%)
  waiting for transfers between devices  25.8 us (20%)
  starting transfers between devices  24.9 us (19%)
  Pallas kernels  14.1 us (11%)
  local copies, waits for them, and re-layouts  3.47 us (3%)
    all_to_all x3, blocking collectives, exchange(): return lax.all_to_all(blocks, axes, 0, 0, tiled=True)  53 us
    all_to_all x2, waiting for transfers between devices, exchange(): return lax.all_to_all(blocks, axes, 0, 0, tiled=True)  24.8 us
    all_to_all x2, starting transfers between devices, exchange(): return lax.all_to_all(blocks, axes, 0, 0, tiled=True)  13.5 us
    all_gather x1, blocking collectives, on_device(): whole = lax.all_gather(across, 'core', axis=0)  7.88 us
    ppermute x1, starting transfers between devices, on_device(): other = lax.ppermute(context, 'core', SWAP)  7.52 us
    pallas_call x1, Pallas kernels, on_device(): pl.pallas_call(attend, out_shape=shape((GROUP, HEAD_DIM + STAT_ROWS, 2 *...  5.47 us
    pallas_call x1, Pallas kernels, on_device(): pl.pallas_call(norm_project, out_shape=(shape((GROUP, ROWS, 256), bf16),...  4.05 us
    ppermute x1, starting transfers between devices, on_device(): w_other = lax.ppermute(w_out, 'core', SWAP)  3.92 us
  transfers between devices with their start and end apart: 4, of which 3 were waited for; matrix products, arithmetic and copies ran while one was open for 1% of the time, Pallas kernels for 6%

profile of v1, /device:TPU:1, one launch (start us, length us, event | category | flops | bytes accessed | tf_op | source)
XLA Modules:
  0.0 130.0 jit_solution(1341815022191233816)
XLA Ops:
  0.0 1.6 %broadcast_in_dim.2 = bf16[4,128,256]{2,1,0:T(8,128)(2,1)} broadcast(bf16[128,256]{1,0:T(8,128)(2,1)} %param.4), dimensions={1,2} | broadcast | bytes 327680 | tf_op jit(solution)/shard_map/broadcast_in_dim | solution.py:120
  1.6 5.4 %all-to-all-start = ((bf16[4,128,256]{2,1,0:T(8,128)(2,1)}), bf16[4,128,256]{2,1,0:T(8,128)(2,1)S(1)}, u32[]{:S(2)}, u32[]{:S(2)}) async-start(bf16[4,128,256]{2,1,0:T(8,128)(2,1)} %broadcast_in_dim.2), calls=%async_computation | async-start | bytes 524288 | tf_op jit(solution)/shard_map/all_to_all | solution.py:124
  7.0 1.3 reshape.4.gain_ref
  8.2 4.3 %all-to-all-done = bf16[4,128,256]{2,1,0:T(8,128)(2,1)S(1)} async-done(((bf16[4,128,256]{2,1,0:T(8,128)(2,1)}), bf16[4,128,256]{2,1,0:T(8,128)(2,1)S(1)}, u32[]{:S(2)}, u32[]{:S(2)}) %all-to-all-start) | async-done | bytes 262176 | tf_op jit(solution)/shard_map/all_to_all | solution.py:124
  12.6 7.9 %all-gather = bf16[8,128,256]{2,1,0:T(8,128)(2,1)} all-gather(bf16[4,128,256]{2,1,0:T(8,128)(2,1)S(1)} %all-to-all-done), channel_id=2, replica_groups=mesh['z'=8,'y_hi'=2,'x'=4,'y_lo'=4,'core'=2] {'core'}, dimensions={0}, use_global_device_ids=true | all-gather | bytes 786432 | tf_op jit(solution)/shard_map/all_gather | solution.py:134
  20.5 0.0 copy-start
  20.5 4.0 %shard_map.46 = (bf16[8,128,256]{2,1,0:T(8,128)(2,1)}, bf16[8,128,512]{2,1,0:T(8,128)(2,1)}) custom-call(bf16[2,4,128,256]{3,2,1,0:T(8,128)(2,1)} %bitcast.1, bf16[8,256]{1,0:T(8,128)(2,1)} %reshape.4.gain_ref, bf16[3,2048,256]{2,1,0:T(8,128)(2,1)} %w_ref.2), custom_call_target="tpu_custom_call" | custom-call | flops 402653184 | bytes 5242880 | tf_op jit(solution)/shard_map/pallas_call | solution.py:135
  24.5 25.0 %all_to_all.25.q_ref = bf16[8,128,256]{2,1,0:T(8,128)(2,1)S(1)} all-to-all(bf16[8,128,256]{2,1,0:T(8,128)(2,1)} %get-tuple-element.7), channel_id=1, replica_groups=mesh['z'=8,'y_hi'=2,'x'=4,'y_lo'=4,'core'=2] {'z'}, dimensions={0} | all-to-all | bytes 1048576 | tf_op jit(solution)/shard_map/all_to_all | solution.py:124
  49.6 8.1 %all-to-all-start.2 = ((bf16[8,128,512]{2,1,0:T(8,128)(2,1)}), bf16[8,128,512]{2,1,0:T(8,128)(2,1)S(1)}, u32[]{:S(2)}, u32[]{:S(2)}) async-start(bf16[8,128,512]{2,1,0:T(8,128)(2,1)} %get-tuple-element.8), calls=%async_computation.2 | async-start | bytes 2097152 | tf_op jit(solution)/shard_map/all_to_all | solution.py:124
  57.6 0.0 copy-done
  57.6 3.9 %collective-permute-start.1 = (bf16[256,2048]{1,0:T(8,128)(2,1)S(1)}, bf16[256,2048]{1,0:T(8,128)(2,1)}, u32[]{:S(2)}, u32[]{:S(2)}) collective-permute-start(bf16[256,2048]{1,0:T(8,128)(2,1)S(1)} %copy-done), channel_id=1, source_target_pairs={{0,1},{1,0},{2,3},{3,2},{4,5},{5,4},{6,7},{7,6},{8,9},{9,8},{10,11... | collective-permute-start | bytes 3145736 | tf_op jit(solution)/shard_map/ppermute | solution.py:133
  61.6 20.4 %all-to-all-done.2.kv_ref = bf16[8,128,512]{2,1,0:T(8,128)(2,1)S(1)} async-done(((bf16[8,128,512]{2,1,0:T(8,128)(2,1)}), bf16[8,128,512]{2,1,0:T(8,128)(2,1)S(1)}, u32[]{:S(2)}, u32[]{:S(2)}) %all-to-all-start.2) | async-done | bytes 1048608 | tf_op jit(solution)/shard_map/all_to_all | solution.py:124
  82.0 5.5 %shard_map.47 = bf16[8,136,256]{2,1,0:T(8,128)(2,1)S(1)} custom-call(bf16[8,128,256]{2,1,0:T(8,128)(2,1)S(1)} %all_to_all.25.q_ref, bf16[8,128,512]{2,1,0:T(8,128)(2,1)S(1)} %all-to-all-done.2.kv_ref), custom_call_target="tpu_custom_call" | custom-call | flops 1073741824 | bytes 3145728 | tf_op jit(solution)/shard_map/pallas_call | solution.py:146
  87.5 0.0 copy-start.1
  87.5 16.7 %all_to_all.26.o_ref = bf16[8,136,256]{2,1,0:T(8,128)(2,1)} all-to-all(bf16[8,136,256]{2,1,0:T(8,128)(2,1)S(1)} %shard_map.47), channel_id=1, replica_groups=mesh['z'=8,'y_hi'=2,'x'=4,'y_lo'=4,'core'=2] {'z'}, dimensions={0} | all-to-all | bytes 1114112 | tf_op jit(solution)/shard_map/all_to_all | solution.py:124
  104.2 1.8 %shard_map.48.own_ref = bf16[128,256]{1,0:T(8,128)(2,1)} custom-call(bf16[8,136,256]{2,1,0:T(8,128)(2,1)} %all_to_all.26.o_ref), custom_call_target="tpu_custom_call" | custom-call | tf_op jit(solution)/shard_map/pallas_call | solution.py:157
  106.0 7.5 %collective-permute-start = (bf16[128,256]{1,0:T(8,128)(2,1)}, bf16[128,256]{1,0:T(8,128)(2,1)S(1)}, u32[]{:S(2)}, u32[]{:S(2)}) collective-permute-start(bf16[128,256]{1,0:T(8,128)(2,1)} %shard_map.48.own_ref), channel_id=1, source_target_pairs={{0,1},{1,0},{2,3},{3,2},{4,5},{5,4},{6,7},{7,6},{8,9},{9,8},{10,11... | collective-permute-start | bytes 196616 | tf_op jit(solution)/shard_map/ppermute | solution.py:163
  113.6 0.0 collective-permute-done.1.w_other_ref
  113.6 1.1 collective-permute-done.other_ref
  114.7 0.6 copy-done.2
  115.3 2.8 %shard_map.49 = bf16[4,128,256]{2,1,0:T(8,128)(2,1)} custom-call(bf16[128,256]{1,0:T(8,128)(2,1)} %shard_map.48.own_ref, bf16[128,256]{1,0:T(8,128)(2,1)} %copy-done.2, bf16[256,2048]{1,0:T(8,128)(2,1)} %w_ref.3, bf16[256,2048]{1,0:T(8,128)(2,1)} %collective-permute-done.1.w_other_ref), custom_call_target="tpu_custom_call" | custom-call | tf_op jit(solution)/shard_map/pallas_call | solution.py:164
  118.1 11.2 %all_to_all.27 = bf16[4,128,256]{2,1,0:T(8,128)(2,1)S(1)} all-to-all(bf16[4,128,256]{2,1,0:T(8,128)(2,1)} %shard_map.49), channel_id=1, replica_groups=mesh['z'=8,'y_hi'=2,'x'=4,'y_lo'=4,'core'=2] {'y_lo'}, dimensions={0} | all-to-all | bytes 524288 | tf_op jit(solution)/shard_map/all_to_all | solution.py:124
  129.3 0.0 copy-done.1
  129.3 0.6 add_convert_fusion
  (2 shorter events, 0.0 us)
Async XLA Ops:
  1.6 11.0 %all-to-all-start = ((bf16[4,128,256]{2,1,0:T(8,128)(2,1)}), bf16[4,128,256]{2,1,0:T(8,128)(2,1)S(1)}, u32[]{:S(2)}, u32[]{:S(2)}) async-start(bf16[4,128,256]{2,1,0:T(8,128)(2,1)} %broadcast_in_dim.2), calls=%async_computation | async-start | bytes 524288 | tf_op jit(solution)/shard_map/all_to_all | solution.py:124
  20.5 37.2 %copy-start = (bf16[256,2048]{1,0:T(8,128)(2,1)S(1)}, bf16[256,2048]{1,0:T(8,128)(2,1)}, u32[]{:S(2)}) copy-start(bf16[256,2048]{1,0:T(8,128)(2,1)} %w_ref.3) | copy-start | bytes 3145732
  49.6 32.4 %all-to-all-start.2 = ((bf16[8,128,512]{2,1,0:T(8,128)(2,1)}), bf16[8,128,512]{2,1,0:T(8,128)(2,1)S(1)}, u32[]{:S(2)}, u32[]{:S(2)}) async-start(bf16[8,128,512]{2,1,0:T(8,128)(2,1)} %get-tuple-element.8), calls=%async_computation.2 | async-start | bytes 2097152 | tf_op jit(solution)/shard_map/all_to_all | solution.py:124
  57.6 55.9 %collective-permute-start.1 = (bf16[256,2048]{1,0:T(8,128)(2,1)S(1)}, bf16[256,2048]{1,0:T(8,128)(2,1)}, u32[]{:S(2)}, u32[]{:S(2)}) collective-permute-start(bf16[256,2048]{1,0:T(8,128)(2,1)S(1)} %copy-done), channel_id=1, source_target_pairs={{0,1},{1,0},{2,3},{3,2},{4,5},{5,4},{6,7},{7,6},{8,9},{9,8},{10,11... | collective-permute-start | bytes 3145736 | tf_op jit(solution)/shard_map/ppermute | solution.py:133
  87.5 41.9 %copy-start.1 = (bf16[128,256]{1,0:T(8,128)(2,1)S(1)}, bf16[128,256]{1,0:T(8,128)(2,1)}, u32[]{:S(2)}) copy-start(bf16[128,256]{1,0:T(8,128)(2,1)} %param.4) | copy-start | bytes 196612
  106.0 8.6 %collective-permute-start = (bf16[128,256]{1,0:T(8,128)(2,1)}, bf16[128,256]{1,0:T(8,128)(2,1)S(1)}, u32[]{:S(2)}, u32[]{:S(2)}) collective-permute-start(bf16[128,256]{1,0:T(8,128)(2,1)} %shard_map.48.own_ref), channel_id=1, source_target_pairs={{0,1},{1,0},{2,3},{3,2},{4,5},{5,4},{6,7},{7,6},{8,9},{9,8},{10,11... | collective-permute-start | bytes 196616 | tf_op jit(solution)/shard_map/ppermute | solution.py:163
  114.7 0.6 copy-start.2

commit v2 on v1

--- a/solution.py
+++ b/solution.py
@@ -50,8 +50,8 @@
     turned = jnp.concatenate(
         [value[:, h * HEAD_DIM : (h + 1) * HEAD_DIM].T for h in range(2)], axis=1
     ).astype(bf16)
+    q_ref[...] = query
     for i in range(GROUP):
-        q_ref[i] = query
         kv_ref[i, :, : 2 * HEAD_DIM] = key
         kv_ref[i, :, 2 * HEAD_DIM :] = turned
 
@@ -100,20 +100,17 @@
     c_ref[...] = total.astype(bf16)
 
 
-def project(own_ref, other_ref, w_ref, w_other_ref, out_ref):
+def project(ctx_ref, w_ref, w_other_ref, out_ref):
     core = lax.axis_index("core")
+    turned = []
+    for c in (core, 1 - core):
+        context = ctx_ref[c]
+        for h in range(2):
+            turned.append(context[:, h * ROWS : (h + 1) * ROWS].T)
+    turned = jnp.concatenate(turned, axis=1)
     for y in range(4):
-        cols = pl.ds(pl.multiple_of((2 * y + core) * 256, 256), 256)
-        total = jnp.zeros((ROWS, 256), f32)
-        for ctx, w in ((own_ref, w_ref), (other_ref, w_other_ref)):
-            for h in range(2):
-                total += lax.dot_general(
-                    ctx[:, h * ROWS : (h + 1) * ROWS],
-                    w[h * HEAD_DIM : (h + 1) * HEAD_DIM, cols],
-                    (((0,), (0,)), ((), ())),
-                    preferred_element_type=f32,
-                )
-        out_ref[y] = total.astype(bf16)
+        weights = jnp.concatenate([w_ref[:, y, :], w_other_ref[:, y, :]], axis=0)
+        out_ref[y] = jnp.dot(turned, weights, preferred_element_type=f32).astype(bf16)
 
 
 def spread(block, count):
@@ -130,19 +127,25 @@
 def on_device(tokens, ln_gain, w_qkv, w_out):
     shape = jax.ShapeDtypeStruct
     across = exchange(spread(tokens, 4), "y_lo")
-    w_other = lax.ppermute(w_out, "core", SWAP)
+    w_cores = w_out.reshape(256, 4, 2, 256)
+    core = lax.axis_index("core")
+    w_own = lax.dynamic_index_in_dim(w_cores, core, 2, keepdims=False)
+    w_other = lax.ppermute(
+        lax.dynamic_index_in_dim(w_cores, 1 - core, 2, keepdims=False), "core", SWAP
+    )
     whole = lax.all_gather(across, "core", axis=0)
-    q_blocks, kv_blocks = pl.pallas_call(
+    query, kv_blocks = pl.pallas_call(
         norm_project,
-        out_shape=(shape((GROUP, ROWS, 256), bf16), shape((GROUP, ROWS, 512), bf16)),
+        out_shape=(shape((ROWS, 256), bf16), shape((GROUP, ROWS, 512), bf16)),
         in_specs=vmem(3),
         out_specs=tuple(vmem(2)),
+        compiler_params=pltpu.CompilerParams(vmem_limit_bytes=24 << 20),
         cost_estimate=pl.CostEstimate(
             flops=2 * ROWS * 2048 * 768, bytes_accessed=5 << 20, transcendentals=0
         ),
     )(whole, ln_gain.reshape(8, 256), w_qkv)
     kv_here = exchange(kv_blocks, ("y_hi", "x"))
-    q_here = exchange(q_blocks, "z")
+    q_here = lax.all_gather(query, "z", axis=0)
     partial = pl.pallas_call(
         attend,
         out_shape=shape((GROUP, HEAD_DIM + STAT_ROWS, 2 * ROWS), bf16),
@@ -159,14 +162,16 @@
         out_shape=shape((HEAD_DIM, 2 * ROWS), bf16),
         in_specs=vmem(1),
         out_specs=vmem(1)[0],
+        compiler_params=pltpu.CompilerParams(vmem_limit_bytes=16 << 20),
     )(shares)
-    other = lax.ppermute(context, "core", SWAP)
+    both = lax.all_gather(context, "core", axis=0)
     projected = pl.pallas_call(
         project,
         out_shape=shape((4, ROWS, 256), bf16),
-        in_specs=vmem(4),
+        in_specs=vmem(3),
         out_specs=vmem(1)[0],
-    )(context, other, w_out, w_other)
+        compiler_params=pltpu.CompilerParams(vmem_limit_bytes=16 << 20),
+    )(both, w_own, w_other)
     summed = jnp.sum(exchange(projected, "y_lo").astype(f32), axis=0)
     return (tokens.astype(f32) + summed).astype(bf16)
 

time: 132 us -> 108 us (0.82)
  waiting for transfers between devices: 25.8 us -> 13.5 us
  blocking collectives: 60.9 us -> 49.8 us
  local copies, waits for them, and re-layouts: 3.47 us -> 7.65 us
  Pallas kernels: 14.1 us -> 10 us
    all_to_all x3 -> x1, blocking collectives: 53 us -> 10.3 us  [exchange(): return lax.all_to_all(blocks, axes, 0, 0, tiled=True)]
    all_gather x0 -> x2, blocking collectives: none -> 31.8 us  [the longest x1 27.4 us: on_device(): q_here = lax.all_gather(query, 'z', axis=0)]
    all_to_all x2 -> x3, waiting for transfers between devices: 24.8 us -> 13.5 us  [exchange(): return lax.all_to_all(blocks, axes, 0, 0, tiled=True)]
    ppermute x2 -> x1, starting transfers between devices: 11.4 us -> 4.18 us  [on_device(): lax.ppermute(lax.dynamic_index_in_dim(w_cores, 1 - core, 2, keepdims=Fals...]
    all_to_all x2 -> x3, starting transfers between devices: 13.5 us -> 20 us  [exchange(): return lax.all_to_all(blocks, axes, 0, 0, tiled=True)]
    pallas_call x1, Pallas kernels: 4.05 us -> 1.84 us  [on_device(): pl.pallas_call(norm_project, out_shape=(shape((ROWS, 256), bf16), shape((...]
    dynamic_slice x0 -> x1, local copies, waits for them, and re-layouts: none -> 2.17 us  [on_device(): lax.dynamic_index_in_dim(w_cores, 1 - core, 2, keepdims=False)]
    unnamed x6 -> x8, local copies, waits for them, and re-layouts: 0.63 us -> 2.44 us
  transfers between devices with their start and end apart: 4 -> 4, of which waited for: 3 -> 2; matrix products, arithmetic and copies ran while one was open for 1% -> 4% of each run, Pallas kernels for 6% -> 0%
where the time goes in v2:
time: 108 us; the launch traced here: 106 us
  blocking collectives  49.8 us (46%)
  starting transfers between devices  24.2 us (22%)
  waiting for transfers between devices  13.5 us (12%)
  Pallas kernels  10 us (9%)
  local copies, waits for them, and re-layouts  7.65 us (7%)
    all_gather x1, blocking collectives, on_device(): q_here = lax.all_gather(query, 'z', axis=0)  27.4 us
    all_to_all x3, starting transfers between devices, exchange(): return lax.all_to_all(blocks, axes, 0, 0, tiled=True)  20 us
    all_to_all x3, waiting for transfers between devices, exchange(): return lax.all_to_all(blocks, axes, 0, 0, tiled=True)  13.5 us
    all_to_all x1, blocking collectives, exchange(): return lax.all_to_all(blocks, axes, 0, 0, tiled=True)  10.3 us
    all_gather x1, blocking collectives, on_device(): whole = lax.all_gather(across, 'core', axis=0)  7.75 us
    pallas_call x1, Pallas kernels, on_device(): pl.pallas_call(attend, out_shape=shape((GROUP, HEAD_DIM + STAT_ROWS, 2 *...  6.27 us
    all_gather x1, blocking collectives, on_device(): both = lax.all_gather(context, 'core', axis=0)  4.4 us
    ppermute x1, starting transfers between devices, on_device(): lax.ppermute(lax.dynamic_index_in_dim(w_cores, 1 - core, 2, keepdims=Fals...  4.18 us
  transfers between devices with their start and end apart: 4, of which 2 were waited for; matrix products, arithmetic and copies ran while one was open for 4% of the time, Pallas kernels for 0%

profile of v2, /device:TPU:1, one launch (start us, length us, event | category | flops | bytes accessed | tf_op | source)
XLA Modules:
  0.0 106.0 jit_solution(5814571733504928268)
XLA Ops:
  0.0 1.6 %broadcast_in_dim.2 = bf16[4,128,256]{2,1,0:T(8,128)(2,1)} broadcast(bf16[128,256]{1,0:T(8,128)(2,1)} %param.4), dimensions={1,2} | broadcast | bytes 327680 | tf_op jit(solution)/shard_map/broadcast_in_dim | solution.py:117
  1.6 5.4 %all-to-all-start = ((bf16[4,128,256]{2,1,0:T(8,128)(2,1)}), bf16[4,128,256]{2,1,0:T(8,128)(2,1)S(1)}, u32[]{:S(2)}, u32[]{:S(2)}) async-start(bf16[4,128,256]{2,1,0:T(8,128)(2,1)} %broadcast_in_dim.2), calls=%async_computation | async-start | bytes 524288 | tf_op jit(solution)/shard_map/all_to_all | solution.py:121
  7.0 0.7 reshape.7.gain_ref
  7.7 4.9 %all-to-all-done = bf16[4,128,256]{2,1,0:T(8,128)(2,1)S(1)} async-done(((bf16[4,128,256]{2,1,0:T(8,128)(2,1)}), bf16[4,128,256]{2,1,0:T(8,128)(2,1)S(1)}, u32[]{:S(2)}, u32[]{:S(2)}) %all-to-all-start) | async-done | bytes 262176 | tf_op jit(solution)/shard_map/all_to_all | solution.py:121
  12.6 7.8 %all-gather = bf16[8,128,256]{2,1,0:T(8,128)(2,1)S(1)} all-gather(bf16[4,128,256]{2,1,0:T(8,128)(2,1)S(1)} %all-to-all-done), channel_id=2, replica_groups=mesh['z'=8,'y_hi'=2,'x'=4,'y_lo'=4,'core'=2] {'core'}, dimensions={0}, use_global_device_ids=true | all-gather | bytes 786432 | tf_op jit(solution)/shard_map/all_gather | solution.py:136
  20.3 1.9 %copy-done = bf16[3,2048,256]{2,1,0:T(8,128)(2,1)S(1)} copy-done((bf16[3,2048,256]{2,1,0:T(8,128)(2,1)S(1)}, bf16[3,2048,256]{2,1,0:T(8,128)(2,1)}, u32[]{:S(2)}) %copy-start) | copy-done | bytes 3145752
  22.2 1.8 %shard_map.46 = (bf16[128,256]{1,0:T(8,128)(2,1)S(1)}, bf16[8,128,512]{2,1,0:T(8,128)(2,1)}) custom-call(bf16[2,4,128,256]{3,2,1,0:T(8,128)(2,1)S(1)} %bitcast.10, bf16[8,256]{1,0:T(8,128)(2,1)S(1)} %reshape.7.gain_ref, bf16[3,2048,256]{2,1,0:T(8,128)(2,1)S(1)} %copy-done), custom_call_target="tpu_custom_call" | custom-call | flops 402653184 | bytes 5242880 | tf_op jit(solution)/shard_map/pallas_call | solution.py:137
  24.1 6.4 %all-to-all-start.1 = ((bf16[8,128,512]{2,1,0:T(8,128)(2,1)}), bf16[8,128,512]{2,1,0:T(8,128)(2,1)S(1)}, u32[]{:S(2)}, u32[]{:S(2)}) async-start(bf16[8,128,512]{2,1,0:T(8,128)(2,1)} %get-tuple-element.8), calls=%async_computation.1 | async-start | bytes 2097152 | tf_op jit(solution)/shard_map/all_to_all | solution.py:121
  30.4 27.4 %all-gather.1 = bf16[1024,256]{1,0:T(8,128)(2,1)S(1)} all-gather(bf16[128,256]{1,0:T(8,128)(2,1)S(1)} %get-tuple-element.7), channel_id=3, replica_groups=mesh['z'=8,'y_hi'=2,'x'=4,'y_lo'=4,'core'=2] {'z'}, dimensions={0}, use_global_device_ids=true | all-gather | bytes 589824 | tf_op jit(solution)/shard_map/all_gather | solution.py:148
  57.8 6.3 %shard_map.47 = bf16[8,136,256]{2,1,0:T(8,128)(2,1)} custom-call(bf16[8,128,256]{2,1,0:T(8,128)(2,1)S(1)} %bitcast.11, bf16[8,128,512]{2,1,0:T(8,128)(2,1)S(1)} %all-to-all-done.1.kv_ref), custom_call_target="tpu_custom_call" | custom-call | flops 1073741824 | bytes 3145728 | tf_op jit(solution)/shard_map/pallas_call | solution.py:149
  64.1 8.3 %all-to-all-start.2 = ((bf16[8,136,256]{2,1,0:T(8,128)(2,1)}), bf16[8,136,256]{2,1,0:T(8,128)(2,1)S(1)}, u32[]{:S(2)}, u32[]{:S(2)}) async-start(bf16[8,136,256]{2,1,0:T(8,128)(2,1)} %shard_map.47), calls=%async_computation.2 | async-start | bytes 1114112 | tf_op jit(solution)/shard_map/all_to_all | solution.py:121
  72.4 0.8 reshape.8
  73.2 2.2 %constant_dynamic-slice_fusion = (bf16[256,4,1,256]{3,2,1,0:T(2,128)(2,1)S(1)}, bf16[256,4,1,256]{3,2,1,0:T(2,128)(2,1)S(1)}) fusion(bf16[256,4,2,256]{3,2,1,0:T(2,128)(2,1)S(1)} %reshape.8, s32[]{:T(128)S(6)} %select_n.8, s32[]{:T(128)S(6)} %select_n.7), kind=kLoop, calls=%fused_computation.4 | loop fusion | bytes 2097160 | tf_op jit(solution)/shard_map/jit(dynamic_index_in_dim)/dynamic_slice | solution.py:134
  75.3 0.0 copy-start.2
  75.4 0.3 copy.13
  75.6 4.2 %collective-permute-start = (bf16[256,4,256]{2,1,0:T(4,128)(2,1)S(1)}, bf16[256,4,256]{2,1,0:T(4,128)(2,1)S(1)}, u32[]{:S(2)}, u32[]{:S(2)}) collective-permute-start(bf16[256,4,256]{2,1,0:T(4,128)(2,1)S(1)} %bitcast.13), channel_id=1, source_target_pairs={{0,1},{1,0},{2,3},{3,2},{4,5},{5,4},{6,7},{7,6},{8,9},{9,8},{10,11... | collective-permute-start | bytes 1572872 | tf_op jit(solution)/shard_map/ppermute | solution.py:133
  79.8 0.3 copy.14
  80.1 8.6 %all-to-all-done.2.o_ref = bf16[8,136,256]{2,1,0:T(8,128)(2,1)S(1)} async-done(((bf16[8,136,256]{2,1,0:T(8,128)(2,1)}), bf16[8,136,256]{2,1,0:T(8,128)(2,1)S(1)}, u32[]{:S(2)}, u32[]{:S(2)}) %all-to-all-start.2) | async-done | bytes 557088 | tf_op jit(solution)/shard_map/all_to_all | solution.py:121
  88.7 0.1 shard_map.48
  88.8 4.4 %all-gather.2 = bf16[256,256]{1,0:T(8,128)(2,1)S(1)} all-gather(bf16[128,256]{1,0:T(8,128)(2,1)S(1)} %shard_map.48), channel_id=4, replica_groups=mesh['z'=8,'y_hi'=2,'x'=4,'y_lo'=4,'core'=2] {'core'}, dimensions={0}, use_global_device_ids=true | all-gather | bytes 196608 | tf_op jit(solution)/shard_map/all_gather | solution.py:167
  93.2 0.0 collective-permute-done.w_other_ref
  93.2 1.8 %shard_map.49 = bf16[4,128,256]{2,1,0:T(8,128)(2,1)S(1)} custom-call(bf16[2,128,256]{2,1,0:T(8,128)(2,1)S(1)} %bitcast.12, bf16[256,4,256]{2,1,0:T(4,128)(2,1)S(1)} %bitcast.9, bf16[256,4,256]{2,1,0:T(4,128)(2,1)S(1)} %collective-permute-done.w_other_ref), custom_call_target="tpu_custom_call" | custom-call | tf_op jit(solution)/shard_map/pallas_call | solution.py:168
  95.0 10.3 %all_to_all.20 = bf16[4,128,256]{2,1,0:T(8,128)(2,1)S(1)} all-to-all(bf16[4,128,256]{2,1,0:T(8,128)(2,1)S(1)} %shard_map.49), channel_id=1, replica_groups=mesh['z'=8,'y_hi'=2,'x'=4,'y_lo'=4,'core'=2] {'y_lo'}, dimensions={0} | all-to-all | bytes 524288 | tf_op jit(solution)/shard_map/all_to_all | solution.py:121
  105.3 0.6 add_convert_fusion
  (6 shorter events, 0.0 us)
Async XLA Ops:
  1.6 11.0 %all-to-all-start = ((bf16[4,128,256]{2,1,0:T(8,128)(2,1)}), bf16[4,128,256]{2,1,0:T(8,128)(2,1)S(1)}, u32[]{:S(2)}, u32[]{:S(2)}) async-start(bf16[4,128,256]{2,1,0:T(8,128)(2,1)} %broadcast_in_dim.2), calls=%async_computation | async-start | bytes 524288 | tf_op jit(solution)/shard_map/all_to_all | solution.py:121
  20.3 1.9 %copy-start = (bf16[3,2048,256]{2,1,0:T(8,128)(2,1)S(1)}, bf16[3,2048,256]{2,1,0:T(8,128)(2,1)}, u32[]{:S(2)}) copy-start(bf16[3,2048,256]{2,1,0:T(8,128)(2,1)} %w_ref.1) | copy-start | bytes 9437188
  24.1 33.7 %all-to-all-start.1 = ((bf16[8,128,512]{2,1,0:T(8,128)(2,1)}), bf16[8,128,512]{2,1,0:T(8,128)(2,1)S(1)}, u32[]{:S(2)}, u32[]{:S(2)}) async-start(bf16[8,128,512]{2,1,0:T(8,128)(2,1)} %get-tuple-element.8), calls=%async_computation.1 | async-start | bytes 2097152 | tf_op jit(solution)/shard_map/all_to_all | solution.py:121
  30.4 41.9 %copy-start.1 = (bf16[256,2048]{1,0:T(8,128)(2,1)S(1)}, bf16[256,2048]{1,0:T(8,128)(2,1)}, u32[]{:S(2)}) copy-start(bf16[256,2048]{1,0:T(8,128)(2,1)} %param.7) | copy-start | bytes 3145732
  64.1 24.6 %all-to-all-start.2 = ((bf16[8,136,256]{2,1,0:T(8,128)(2,1)}), bf16[8,136,256]{2,1,0:T(8,128)(2,1)S(1)}, u32[]{:S(2)}, u32[]{:S(2)}) async-start(bf16[8,136,256]{2,1,0:T(8,128)(2,1)} %shard_map.47), calls=%async_computation.2 | async-start | bytes 1114112 | tf_op jit(solution)/shard_map/all_to_all | solution.py:121
  75.3 30.0 %copy-start.2 = (bf16[128,256]{1,0:T(8,128)(2,1)S(1)}, bf16[128,256]{1,0:T(8,128)(2,1)}, u32[]{:S(2)}) copy-start(bf16[128,256]{1,0:T(8,128)(2,1)} %param.4) | copy-start | bytes 196612
  75.6 17.6 %collective-permute-start = (bf16[256,4,256]{2,1,0:T(4,128)(2,1)S(1)}, bf16[256,4,256]{2,1,0:T(4,128)(2,1)S(1)}, u32[]{:S(2)}, u32[]{:S(2)}) collective-permute-start(bf16[256,4,256]{2,1,0:T(4,128)(2,1)S(1)} %bitcast.13), channel_id=1, source_target_pairs={{0,1},{1,0},{2,3},{3,2},{4,5},{5,4},{6,7},{7,6},{8,9},{9,8},{10,11... | collective-permute-start | bytes 1572872 | tf_op jit(solution)/shard_map/ppermute | solution.py:133

commit v3 on v2

v3 whole, which is shorter than its diff:
```python
import functools
import math

import jax
import jax.numpy as jnp
from jax import lax
from jax.experimental import pallas as pl
from jax.experimental.pallas import tpu as pltpu
from jax.sharding import Mesh
from jax.sharding import PartitionSpec as P

HEAD_DIM = 128
ROWS = 128
STAT_ROWS = 8
LOG2E = math.log2(math.e)
QUERY_GROUP = 8
KEY_GROUP = 4
SWAP = ((0, 1), (1, 0))
bf16 = jnp.bfloat16
f32 = jnp.float32
shape = jax.ShapeDtypeStruct


def vmem(count):
    return [pl.BlockSpec(memory_space=pltpu.VMEM)] * count


def limit(mib):
    return pltpu.CompilerParams(vmem_limit_bytes=mib << 20)


def repeat(tokens_ref, copies_ref):
    for i in range(4):
        copies_ref[i] = tokens_ref[...]


def norm_project(x_ref, gain_ref, w_ref, q_ref, kv_ref):
    width = x_ref.shape[3]
    gains = gain_ref[...].astype(f32).reshape(8, 256)
    blocks = [(y, c) for y in range(4) for c in range(2)]
    total = jnp.zeros((ROWS, width), f32)
    squares = jnp.zeros((ROWS, width), f32)
    for y, c in blocks:
        part = x_ref[c, y].astype(f32)
        total += part
        squares += part * part
    features = width * len(blocks)
    average = jnp.sum(total, axis=1, keepdims=True) / features
    second = jnp.sum(squares, axis=1, keepdims=True) / features
    inverse = lax.rsqrt(second - average * average + 1e-6)
    sums = [jnp.zeros((ROWS, width), f32) for _ in range(3)]
    for t, (y, c) in enumerate(blocks):
        part = x_ref[c, y].astype(f32)
        gain = gains[t : t + 1, :]
        normed = ((part - average) * inverse * gain).astype(bf16)
        for j in range(3):
            sums[j] += jnp.dot(
                normed, w_ref[j, t * width : (t + 1) * width, :], preferred_element_type=f32
            )
    query = sums[0].astype(bf16)
    q_ref[...] = query
    keys = sums[1].astype(bf16)
    turned = jnp.concatenate([sums[2][:, :HEAD_DIM].T, sums[2][:, HEAD_DIM:].T], axis=1).astype(bf16)
    for i in range(8):
        kv_ref[i, :, :256] = keys
        kv_ref[i, :, 256:] = turned


def attend(q_ref, kv_ref, o_ref):
    factor = HEAD_DIM**-0.5 * LOG2E
    for h in range(2):
        cols = slice(h * HEAD_DIM, (h + 1) * HEAD_DIM)
        vcols = slice((2 + h) * HEAD_DIM, (3 + h) * HEAD_DIM)
        keys = kv_ref[:, :, cols].reshape(2 * KEY_GROUP * ROWS, HEAD_DIM)
        values = jnp.concatenate(
            [
                kv_ref[s, a * ROWS : (a + 1) * ROWS, vcols]
                for s in range(KEY_GROUP)
                for a in range(2)
            ],
            axis=1,
        )
        for pair in range(QUERY_GROUP // 2):
            query = q_ref[2 * pair : 2 * pair + 2, :, cols].reshape(2 * ROWS, HEAD_DIM)
            scores = lax.dot_general(
                keys, query, (((1,), (1,)), ((), ())), preferred_element_type=f32
            )
            highest = jnp.max(scores, axis=0, keepdims=True)
            expon = jnp.exp2((scores - highest) * factor)
            denom = jnp.sum(expon, axis=0, keepdims=True)
            context = jnp.dot(values, expon.astype(bf16), preferred_element_type=f32)
            context = (context / denom).astype(bf16)
            level = highest * factor + jnp.log2(denom)
            first = level.astype(bf16).astype(f32)
            middle = (level - first).astype(bf16).astype(f32)
            last = level - first - middle
            stats = jnp.concatenate(
                [first, middle, last, jnp.zeros((STAT_ROWS - 3, 2 * ROWS), f32)], axis=0
            ).astype(bf16)
            for i in range(2):
                span = slice(i * ROWS, (i + 1) * ROWS)
                o_ref[2 * pair + i, :HEAD_DIM, cols] = context[:, span]
                o_ref[2 * pair + i, HEAD_DIM:, cols] = stats[:, span]


def combine(o_ref, c_ref):
    levels = []
    for s in range(QUERY_GROUP):
        stats = o_ref[s, HEAD_DIM:, :].astype(f32)
        levels.append(stats[0:1] + stats[1:2] + stats[2:3])
    highest = functools.reduce(jnp.maximum, levels)
    shares = [jnp.exp2(level - highest) for level in levels]
    denom = functools.reduce(jnp.add, shares)
    total = jnp.zeros((HEAD_DIM, 2 * ROWS), f32)
    for s in range(QUERY_GROUP):
        total += o_ref[s, :HEAD_DIM, :].astype(f32) * (shares[s] / denom)
    c_ref[...] = total.astype(bf16)


def project(ctx_ref, w_ref, w_other_ref, out_ref):
    core = lax.axis_index("core")
    turned = []
    for c in (core, 1 - core):
        context = ctx_ref[c]
        for h in range(2):
            turned.append(context[:, h * ROWS : (h + 1) * ROWS].T)
    turned = jnp.concatenate(turned, axis=1)
    for y in range(4):
        cols = pl.ds(pl.multiple_of((2 * y + core) * 256, 256), 256)
        weights = jnp.concatenate([w_ref[:, cols], w_other_ref[:, cols]], axis=0)
        out_ref[y] = jnp.dot(turned, weights, preferred_element_type=f32).astype(bf16)


def exchange(blocks, axes):
    return lax.all_to_all(blocks, axes, 0, 0, tiled=True)


def on_device(tokens, ln_gain, w_qkv, w_out):
    copies = pl.pallas_call(
        repeat,
        out_shape=shape((4, *tokens.shape), bf16),
        in_specs=vmem(1),
        out_specs=vmem(1)[0],
        compiler_params=limit(4),
    )(tokens)
    across = exchange(copies, "y_lo")
    w_other = lax.ppermute(w_out, "core", SWAP)
    whole = lax.all_gather(across, "core", axis=0)
    q_blocks, kv_near = pl.pallas_call(
        norm_project,
        out_shape=(shape((ROWS, 256), bf16), shape((8, ROWS, 512), bf16)),
        in_specs=vmem(3),
        out_specs=tuple(vmem(2)),
        compiler_params=limit(24),
        cost_estimate=pl.CostEstimate(
            flops=2 * ROWS * 2048 * 768, bytes_accessed=5 << 20, transcendentals=0
        ),
    )(whole, ln_gain, w_qkv)
    kv_here = exchange(kv_near, ("y_hi", "x")).reshape(4, 256, 512)
    q_here = lax.all_gather(q_blocks, "z", axis=0)
    partial = pl.pallas_call(
        attend,
        out_shape=shape((QUERY_GROUP, HEAD_DIM + STAT_ROWS, 2 * ROWS), bf16),
        in_specs=vmem(2),
        out_specs=vmem(1)[0],
        compiler_params=limit(24),
        cost_estimate=pl.CostEstimate(
            flops=4 * 1024 * 1024 * 256, bytes_accessed=3 << 20, transcendentals=2 << 20
        ),
    )(q_here, kv_here)
    shares = exchange(partial, "z")
    context = pl.pallas_call(
        combine,
        out_shape=shape((HEAD_DIM, 2 * ROWS), bf16),
        in_specs=vmem(1),
        out_specs=vmem(1)[0],
        compiler_params=limit(16),
    )(shares)
    projected = pl.pallas_call(
        project,
        out_shape=shape((4, ROWS, 256), bf16),
        in_specs=vmem(3),
        out_specs=vmem(1)[0],
        compiler_params=limit(16),
    )(lax.all_gather(context, "core", axis=0), w_out, w_other)
    summed = jnp.sum(exchange(projected, "y_lo").astype(f32), axis=0)
    return (tokens.astype(f32) + summed).astype(bf16)


def solution(mesh):
    grid = Mesh(mesh.devices.reshape(8, 2, 4, 4, 2), ("z", "y_hi", "x", "y_lo", "core"))
    seq, tp = ("z", "y_hi", "x"), ("y_lo", "core")
    return jax.shard_map(
        on_device,
        mesh=grid,
        in_specs=(P(seq, tp), P(), P(None, None, tp), P(tp, None)),
        out_specs=P(seq, tp),
        check_vma=False,
    )
```

time: 108 us -> 106 us (0.981)
  blocking collectives: 49.8 us -> 82.5 us
  starting transfers between devices: 24.2 us -> 8.52 us
  waiting for transfers between devices: 13.5 us -> 0.01 us
  local copies, waits for them, and re-layouts: 7.65 us -> 4.47 us
  Pallas kernels: 10 us -> 7.81 us
    all_to_all x1 -> x3, blocking collectives: 10.3 us -> 39.4 us  [exchange(): return lax.all_to_all(blocks, axes, 0, 0, tiled=True)]
    all_to_all x3 -> x1, starting transfers between devices: 20 us -> 5.96 us  [exchange(): return lax.all_to_all(blocks, axes, 0, 0, tiled=True)]
    all_to_all x3 -> x1, waiting for transfers between devices: 13.5 us -> 0.01 us  [exchange(): return lax.all_to_all(blocks, axes, 0, 0, tiled=True)]
    all_gather x2, blocking collectives: 31.8 us -> 36.1 us  [the longest x1 28.8 us: on_device(): q_here = lax.all_gather(q_blocks, 'z', axis=0)]
    dynamic_slice x1 -> x0, local copies, waits for them, and re-layouts: 2.17 us -> none  [on_device(): lax.dynamic_index_in_dim(w_cores, 1 - core, 2, keepdims=False)]
    unnamed x8 -> x12, local copies, waits for them, and re-layouts: 2.44 us -> 4.47 us
    ppermute x1, starting transfers between devices: 4.18 us -> 2.56 us  [on_device(): w_other = lax.ppermute(w_out, 'core', SWAP)]
    broadcast_in_dim x1 -> x0, local copies, waits for them, and re-layouts: 1.55 us -> none  [spread(): return jnp.broadcast_to(block[None], (count, *block.shape))]
  transfers between devices with their start and end apart: 4 -> 2, of which waited for: 2 -> 0; matrix products, arithmetic and copies ran while one was open for 4% -> 0% of each run, Pallas kernels for 0% -> 5%
where the time goes in v3:
time: 106 us; the launch traced here: 104 us
  blocking collectives  82.5 us (78%)
  starting transfers between devices  8.52 us (8%)
  Pallas kernels  7.81 us (7%)
  local copies, waits for them, and re-layouts  4.47 us (4%)
    all_to_all x3, blocking collectives, exchange(): return lax.all_to_all(blocks, axes, 0, 0, tiled=True)  39.4 us
    all_gather x1, blocking collectives, on_device(): q_here = lax.all_gather(q_blocks, 'z', axis=0)  28.8 us
    all_gather x1, blocking collectives, on_device(): lax.all_gather(context, 'core', axis=0)  7.32 us
    all_gather x1, blocking collectives, on_device(): whole = lax.all_gather(across, 'core', axis=0)  6.96 us
    all_to_all x1, starting transfers between devices, exchange(): return lax.all_to_all(blocks, axes, 0, 0, tiled=True)  5.96 us
    pallas_call x1, Pallas kernels, on_device(): pl.pallas_call(attend, out_shape=shape((QUERY_GROUP, HEAD_DIM + STAT_ROWS...  5.47 us
    unnamed x12, local copies, waits for them, and re-layouts  4.47 us
    ppermute x1, starting transfers between devices, on_device(): w_other = lax.ppermute(w_out, 'core', SWAP)  2.56 us
  transfers between devices with their start and end apart: 2, of which 0 were waited for; matrix products, arithmetic and copies ran while one was open for 0% of the time, Pallas kernels for 5%

profile of v3, /device:TPU:1, one launch (start us, length us, event | category | flops | bytes accessed | tf_op | source)
XLA Modules:
  0.0 104.0 jit_solution(640386100384273440)
XLA Ops:
  0.0 0.8 copy-done.3
  0.9 0.0 copy-start.1
  0.9 11.3 %all_to_all.20 = bf16[4,128,256]{2,1,0:T(8,128)(2,1)S(1)} all-to-all(bf16[4,128,256]{2,1,0:T(8,128)(2,1)S(1)} %shard_map.46), channel_id=1, replica_groups=mesh['z'=8,'y_hi'=2,'x'=4,'y_lo'=4,'core'=2] {'y_lo'}, dimensions={0} | all-to-all | bytes 524288 | tf_op jit(solution)/shard_map/all_to_all | solution.py:135
  12.2 7.0 %all-gather = bf16[8,128,256]{2,1,0:T(8,128)(2,1)S(1)} all-gather(bf16[4,128,256]{2,1,0:T(8,128)(2,1)S(1)} %all_to_all.20), channel_id=2, replica_groups=mesh['z'=8,'y_hi'=2,'x'=4,'y_lo'=4,'core'=2] {'core'}, dimensions={0}, use_global_device_ids=true | all-gather | bytes 786432 | tf_op jit(solution)/shard_map/all_gather | solution.py:148
  19.2 0.0 copy-start
  19.2 1.9 %copy-done = bf16[3,2048,256]{2,1,0:T(8,128)(2,1)S(1)} copy-done((bf16[3,2048,256]{2,1,0:T(8,128)(2,1)S(1)}, bf16[3,2048,256]{2,1,0:T(8,128)(2,1)}, u32[]{:S(2)}) %copy-start) | copy-done | bytes 3145752
  21.0 0.7 copy-done.5
  21.7 1.8 %shard_map.47 = (bf16[128,256]{1,0:T(8,128)(2,1)S(1)}, bf16[8,128,512]{2,1,0:T(8,128)(2,1)}) custom-call(bf16[2,4,128,256]{3,2,1,0:T(8,128)(2,1)S(1)} %bitcast.4, bf16[2048]{0:T(1024)(128)(2,1)S(1)} %copy-done.5, bf16[3,2048,256]{2,1,0:T(8,128)(2,1)S(1)} %copy-done), custom_call_target="tpu_custom_call" | custom-call | flops 402653184 | bytes 5242880 | tf_op jit(solution)/shard_map/pallas_call | solution.py:149
  23.6 6.0 %all-to-all-start.1 = ((bf16[8,128,512]{2,1,0:T(8,128)(2,1)}), bf16[8,128,512]{2,1,0:T(8,128)(2,1)S(1)}, u32[]{:S(2)}, u32[]{:S(2)}) async-start(bf16[8,128,512]{2,1,0:T(8,128)(2,1)} %get-tuple-element.8), calls=%async_computation.1 | async-start | bytes 2097152 | tf_op jit(solution)/shard_map/all_to_all | solution.py:135
  29.5 0.0 copy-done.1
  29.5 2.6 %collective-permute-start = (bf16[256,2048]{1,0:T(8,128)(2,1)S(1)}, bf16[256,2048]{1,0:T(8,128)(2,1)S(1)}, u32[]{:S(2)}, u32[]{:S(2)}) collective-permute-start(bf16[256,2048]{1,0:T(8,128)(2,1)S(1)} %copy-done.1), channel_id=1, source_target_pairs={{0,1},{1,0},{2,3},{3,2},{4,5},{5,4},{6,7},{7,6},{8,9},{9,8},{10,11... | collective-permute-start | bytes 3145736 | tf_op jit(solution)/shard_map/ppermute | solution.py:147
  32.1 28.8 %all-gather.1 = bf16[1024,256]{1,0:T(8,128)(2,1)} all-gather(bf16[128,256]{1,0:T(8,128)(2,1)S(1)} %get-tuple-element.7), channel_id=3, replica_groups=mesh['z'=8,'y_hi'=2,'x'=4,'y_lo'=4,'core'=2] {'z'}, dimensions={0}, use_global_device_ids=true | all-gather | bytes 589824 | tf_op jit(solution)/shard_map/all_gather | solution.py:160
  60.9 0.0 all-to-all-done.1
  60.9 1.0 %copy-done.2 = bf16[1024,256]{1,0:T(8,128)(2,1)S(1)} copy-done((bf16[1024,256]{1,0:T(8,128)(2,1)S(1)}, bf16[1024,256]{1,0:T(8,128)(2,1)}, u32[]{:S(2)}) %copy-start.2) | copy-done | bytes 524312
  62.0 5.5 %shard_map.48 = bf16[8,136,256]{2,1,0:T(8,128)(2,1)S(1)} custom-call(bf16[8,128,256]{2,1,0:T(8,128)(2,1)S(1)} %bitcast.7, bf16[4,256,512]{2,1,0:T(8,128)(2,1)S(1)} %bitcast.5), custom_call_target="tpu_custom_call" | custom-call | flops 1073741824 | bytes 3145728 | tf_op jit(solution)/shard_map/pallas_call | solution.py:161
  67.4 0.0 copy-start.4
  67.4 18.0 %all_to_all.21.o_ref = bf16[8,136,256]{2,1,0:T(8,128)(2,1)S(1)} all-to-all(bf16[8,136,256]{2,1,0:T(8,128)(2,1)S(1)} %shard_map.48), channel_id=1, replica_groups=mesh['z'=8,'y_hi'=2,'x'=4,'y_lo'=4,'core'=2] {'z'}, dimensions={0} | all-to-all | bytes 1114112 | tf_op jit(solution)/shard_map/all_to_all | solution.py:135
  85.5 0.1 shard_map.49
  85.6 7.3 %all-gather.2 = bf16[256,256]{1,0:T(8,128)(2,1)S(1)} all-gather(bf16[128,256]{1,0:T(8,128)(2,1)S(1)} %shard_map.49), channel_id=4, replica_groups=mesh['z'=8,'y_hi'=2,'x'=4,'y_lo'=4,'core'=2] {'core'}, dimensions={0}, use_global_device_ids=true | all-gather | bytes 196608 | tf_op jit(solution)/shard_map/all_gather | solution.py:185
  92.9 0.0 collective-permute-done.w_other_ref
  92.9 0.3 shard_map.50
  93.3 10.0 %all_to_all.22 = bf16[4,128,256]{2,1,0:T(8,128)(2,1)S(1)} all-to-all(bf16[4,128,256]{2,1,0:T(8,128)(2,1)S(1)} %shard_map.50), channel_id=1, replica_groups=mesh['z'=8,'y_hi'=2,'x'=4,'y_lo'=4,'core'=2] {'y_lo'}, dimensions={0} | all-to-all | bytes 524288 | tf_op jit(solution)/shard_map/all_to_all | solution.py:135
  103.4 0.0 copy-done.4
  103.4 0.6 add_convert_fusion
  (5 shorter events, 0.1 us)
Async XLA Ops:
  0.0 0.8 copy-start.3
  0.9 28.7 %copy-start.1 = (bf16[256,2048]{1,0:T(8,128)(2,1)S(1)}, bf16[256,2048]{1,0:T(8,128)(2,1)}, u32[]{:S(2)}) copy-start(bf16[256,2048]{1,0:T(8,128)(2,1)} %w_ref.3) | copy-start | bytes 3145732
  19.2 1.9 %copy-start = (bf16[3,2048,256]{2,1,0:T(8,128)(2,1)S(1)}, bf16[3,2048,256]{2,1,0:T(8,128)(2,1)}, u32[]{:S(2)}) copy-start(bf16[3,2048,256]{2,1,0:T(8,128)(2,1)} %w_ref.2) | copy-start | bytes 9437188
  21.0 0.7 copy-start.5
  23.6 37.3 %all-to-all-start.1 = ((bf16[8,128,512]{2,1,0:T(8,128)(2,1)}), bf16[8,128,512]{2,1,0:T(8,128)(2,1)S(1)}, u32[]{:S(2)}, u32[]{:S(2)}) async-start(bf16[8,128,512]{2,1,0:T(8,128)(2,1)} %get-tuple-element.8), calls=%async_computation.1 | async-start | bytes 2097152 | tf_op jit(solution)/shard_map/all_to_all | solution.py:135
  29.5 63.4 %collective-permute-start = (bf16[256,2048]{1,0:T(8,128)(2,1)S(1)}, bf16[256,2048]{1,0:T(8,128)(2,1)S(1)}, u32[]{:S(2)}, u32[]{:S(2)}) collective-permute-start(bf16[256,2048]{1,0:T(8,128)(2,1)S(1)} %copy-done.1), channel_id=1, source_target_pairs={{0,1},{1,0},{2,3},{3,2},{4,5},{5,4},{6,7},{7,6},{8,9},{9,8},{10,11... | collective-permute-start | bytes 3145736 | tf_op jit(solution)/shard_map/ppermute | solution.py:147
  60.9 1.0 %copy-start.2 = (bf16[1024,256]{1,0:T(8,128)(2,1)S(1)}, bf16[1024,256]{1,0:T(8,128)(2,1)}, u32[]{:S(2)}) copy-start(bf16[1024,256]{1,0:T(8,128)(2,1)} %all-gather.1) | copy-start | bytes 1572868
  67.4 35.9 %copy-start.4 = (bf16[128,256]{1,0:T(8,128)(2,1)S(1)}, bf16[128,256]{1,0:T(8,128)(2,1)}, u32[]{:S(2)}) copy-start(bf16[128,256]{1,0:T(8,128)(2,1)} %tokens_ref.1) | copy-start | bytes 196612

commit v4 on v3

--- a/solution.py
+++ b/solution.py
@@ -34,7 +34,8 @@
         copies_ref[i] = tokens_ref[...]
 
 
-def norm_project(x_ref, gain_ref, w_ref, q_ref, kv_ref):
+def norm_project(x_ref, gain_ref, wq_ref, wk_ref, wv_ref, q_ref, kv_ref):
+    w_refs = (wq_ref, wk_ref, wv_ref)
     width = x_ref.shape[3]
     gains = gain_ref[...].astype(f32).reshape(8, 256)
     blocks = [(y, c) for y in range(4) for c in range(2)]
@@ -55,7 +56,7 @@
         normed = ((part - average) * inverse * gain).astype(bf16)
         for j in range(3):
             sums[j] += jnp.dot(
-                normed, w_ref[j, t * width : (t + 1) * width, :], preferred_element_type=f32
+                normed, w_refs[j][t * width : (t + 1) * width, :], preferred_element_type=f32
             )
     query = sums[0].astype(bf16)
     q_ref[...] = query
@@ -149,13 +150,13 @@
     q_blocks, kv_near = pl.pallas_call(
         norm_project,
         out_shape=(shape((ROWS, 256), bf16), shape((8, ROWS, 512), bf16)),
-        in_specs=vmem(3),
+        in_specs=vmem(5),
         out_specs=tuple(vmem(2)),
         compiler_params=limit(24),
         cost_estimate=pl.CostEstimate(
             flops=2 * ROWS * 2048 * 768, bytes_accessed=5 << 20, transcendentals=0
         ),
-    )(whole, ln_gain, w_qkv)
+    )(whole, ln_gain, w_qkv[0], w_qkv[1], w_qkv[2])
     kv_here = exchange(kv_near, ("y_hi", "x")).reshape(4, 256, 512)
     q_here = lax.all_gather(q_blocks, "z", axis=0)
     partial = pl.pallas_call(

time: 106 us -> 105 us (level)
  blocking collectives: 82.5 us -> 71.7 us
  starting transfers between devices: 8.52 us -> 14.3 us
  waiting for transfers between devices: 0.01 us -> 3.56 us
    all_to_all x3 -> x2, blocking collectives: 39.4 us -> 26.6 us  [exchange(): return lax.all_to_all(blocks, axes, 0, 0, tiled=True)]
    all_to_all x1 -> x2, starting transfers between devices: 5.96 us -> 11.8 us  [exchange(): return lax.all_to_all(blocks, axes, 0, 0, tiled=True)]
    all_to_all x1 -> x2, waiting for transfers between devices: 0.01 us -> 3.55 us  [exchange(): return lax.all_to_all(blocks, axes, 0, 0, tiled=True)]
    squeeze x0 -> x1, local copies, waits for them, and re-layouts: none -> 2.07 us  [on_device(): w_qkv[2]]
    unnamed x12, local copies, waits for them, and re-layouts: 4.47 us -> 2.87 us
  transfers between devices with their start and end apart: 2 -> 3, of which waited for: 0 -> 1; matrix products, arithmetic and copies ran while one was open for 0% -> 2% of each run, Pallas kernels for 5% -> 5%
where the time goes in v4:
time: 105 us; the launch traced here: 103 us
  blocking collectives  71.7 us (68%)
  starting transfers between devices  14.3 us (14%)
  Pallas kernels  7.52 us (7%)
  local copies, waits for them, and re-layouts  4.94 us (5%)
  waiting for transfers between devices  3.56 us (3%)
    all_gather x1, blocking collectives, on_device(): q_here = lax.all_gather(q_blocks, 'z', axis=0)  29 us
    all_to_all x2, blocking collectives, exchange(): return lax.all_to_all(blocks, axes, 0, 0, tiled=True)  26.6 us
    all_to_all x2, starting transfers between devices, exchange(): return lax.all_to_all(blocks, axes, 0, 0, tiled=True)  11.8 us
    all_gather x1, blocking collectives, on_device(): lax.all_gather(context, 'core', axis=0)  8.31 us
    all_gather x1, blocking collectives, on_device(): whole = lax.all_gather(across, 'core', axis=0)  7.75 us
    pallas_call x1, Pallas kernels, on_device(): pl.pallas_call(attend, out_shape=shape((QUERY_GROUP, HEAD_DIM + STAT_ROWS...  5.47 us
    all_to_all x2, waiting for transfers between devices, exchange(): return lax.all_to_all(blocks, axes, 0, 0, tiled=True)  3.55 us
    unnamed x12, local copies, waits for them, and re-layouts  2.87 us
  transfers between devices with their start and end apart: 3, of which 1 were waited for; matrix products, arithmetic and copies ran while one was open for 2% of the time, Pallas kernels for 5%

profile of v4, /device:TPU:1, one launch (start us, length us, event | category | flops | bytes accessed | tf_op | source)
XLA Modules:
  0.0 102.8 jit_solution(15678694400599665883)
XLA Ops:
  0.0 0.8 copy-done.3
  0.8 0.7 shard_map.46
  1.6 5.4 %all-to-all-start = ((bf16[4,128,256]{2,1,0:T(8,128)(2,1)}), bf16[4,128,256]{2,1,0:T(8,128)(2,1)S(1)}, u32[]{:S(2)}, u32[]{:S(2)}) async-start(bf16[4,128,256]{2,1,0:T(8,128)(2,1)} %shard_map.46), calls=%async_computation | async-start | bytes 524288 | tf_op jit(solution)/shard_map/all_to_all | solution.py:136
  7.0 2.1 %slice_bitcast_fusion = (bf16[2048,256]{1,0:T(8,128)(2,1)S(1)}, bf16[2048,256]{1,0:T(8,128)(2,1)S(1)}, bf16[2048,256]{1,0:T(8,128)(2,1)S(1)}) fusion(bf16[3,2048,256]{2,1,0:T(8,128)(2,1)} %param.6), kind=kLoop, calls=%fused_computation | loop fusion | bytes 6291456 | tf_op jit(solution)/shard_map/squeeze | solution.py:159
  9.1 3.5 %all-to-all-done = bf16[4,128,256]{2,1,0:T(8,128)(2,1)S(1)} async-done(((bf16[4,128,256]{2,1,0:T(8,128)(2,1)}), bf16[4,128,256]{2,1,0:T(8,128)(2,1)S(1)}, u32[]{:S(2)}, u32[]{:S(2)}) %all-to-all-start) | async-done | bytes 262176 | tf_op jit(solution)/shard_map/all_to_all | solution.py:136
  12.6 7.8 %all-gather = bf16[8,128,256]{2,1,0:T(8,128)(2,1)S(1)} all-gather(bf16[4,128,256]{2,1,0:T(8,128)(2,1)S(1)} %all-to-all-done), channel_id=2, replica_groups=mesh['z'=8,'y_hi'=2,'x'=4,'y_lo'=4,'core'=2] {'core'}, dimensions={0}, use_global_device_ids=true | all-gather | bytes 786432 | tf_op jit(solution)/shard_map/all_gather | solution.py:149
  20.4 0.8 shard_map.47
  21.2 0.0 copy-start.1
  21.2 1.0 copy-done.1
  22.2 6.4 %all-to-all-start.1 = ((bf16[8,128,512]{2,1,0:T(8,128)(2,1)}), bf16[8,128,512]{2,1,0:T(8,128)(2,1)S(1)}, u32[]{:S(2)}, u32[]{:S(2)}) async-start(bf16[8,128,512]{2,1,0:T(8,128)(2,1)} %copy-done.1), calls=%async_computation.1 | async-start | bytes 2097152 | tf_op jit(solution)/shard_map/all_to_all | solution.py:136
  28.5 2.6 %collective-permute-start = (bf16[256,2048]{1,0:T(8,128)(2,1)}, bf16[256,2048]{1,0:T(8,128)(2,1)S(1)}, u32[]{:S(2)}, u32[]{:S(2)}) collective-permute-start(bf16[256,2048]{1,0:T(8,128)(2,1)} %w_ref.1), channel_id=1, source_target_pairs={{0,1},{1,0},{2,3},{3,2},{4,5},{5,4},{6,7},{7,6},{8,9},{9,8},{10,11... | collective-permute-start | bytes 3145736 | tf_op jit(solution)/shard_map/ppermute | solution.py:148
  31.1 0.0 copy-start
  31.1 29.0 %all-gather.1 = bf16[1024,256]{1,0:T(8,128)(2,1)} all-gather(bf16[128,256]{1,0:T(8,128)(2,1)S(1)} %get-tuple-element.7), channel_id=3, replica_groups=mesh['z'=8,'y_hi'=2,'x'=4,'y_lo'=4,'core'=2] {'z'}, dimensions={0}, use_global_device_ids=true | all-gather | bytes 589824 | tf_op jit(solution)/shard_map/all_gather | solution.py:161
  60.2 0.0 all-to-all-done.1
  60.2 1.0 %copy-done.2 = bf16[1024,256]{1,0:T(8,128)(2,1)S(1)} copy-done((bf16[1024,256]{1,0:T(8,128)(2,1)S(1)}, bf16[1024,256]{1,0:T(8,128)(2,1)}, u32[]{:S(2)}) %copy-start.2) | copy-done | bytes 524312
  61.2 5.5 %shard_map.48 = bf16[8,136,256]{2,1,0:T(8,128)(2,1)S(1)} custom-call(bf16[8,128,256]{2,1,0:T(8,128)(2,1)S(1)} %bitcast.13, bf16[4,256,512]{2,1,0:T(8,128)(2,1)S(1)} %bitcast.11), custom_call_target="tpu_custom_call" | custom-call | flops 1073741824 | bytes 3145728 | tf_op jit(solution)/shard_map/pallas_call | solution.py:162
  66.7 0.0 copy-start.4
  66.7 16.4 %all_to_all.20.o_ref = bf16[8,136,256]{2,1,0:T(8,128)(2,1)S(1)} all-to-all(bf16[8,136,256]{2,1,0:T(8,128)(2,1)S(1)} %shard_map.48), channel_id=1, replica_groups=mesh['z'=8,'y_hi'=2,'x'=4,'y_lo'=4,'core'=2] {'z'}, dimensions={0} | all-to-all | bytes 1114112 | tf_op jit(solution)/shard_map/all_to_all | solution.py:136
  83.1 0.1 shard_map.49
  83.2 8.3 %all-gather.2 = bf16[256,256]{1,0:T(8,128)(2,1)S(1)} all-gather(bf16[128,256]{1,0:T(8,128)(2,1)S(1)} %shard_map.49), channel_id=4, replica_groups=mesh['z'=8,'y_hi'=2,'x'=4,'y_lo'=4,'core'=2] {'core'}, dimensions={0}, use_global_device_ids=true | all-gather | bytes 196608 | tf_op jit(solution)/shard_map/all_gather | solution.py:186
  91.5 0.0 collective-permute-done.w_other_ref
  91.5 0.3 shard_map.50
  91.9 10.3 %all_to_all.21 = bf16[4,128,256]{2,1,0:T(8,128)(2,1)S(1)} all-to-all(bf16[4,128,256]{2,1,0:T(8,128)(2,1)S(1)} %shard_map.50), channel_id=1, replica_groups=mesh['z'=8,'y_hi'=2,'x'=4,'y_lo'=4,'core'=2] {'y_lo'}, dimensions={0} | all-to-all | bytes 524288 | tf_op jit(solution)/shard_map/all_to_all | solution.py:136
  102.2 0.6 add_convert_fusion
  (7 shorter events, 0.0 us)
Async XLA Ops:
  0.0 0.8 copy-start.3
  1.6 11.0 %all-to-all-start = ((bf16[4,128,256]{2,1,0:T(8,128)(2,1)}), bf16[4,128,256]{2,1,0:T(8,128)(2,1)S(1)}, u32[]{:S(2)}, u32[]{:S(2)}) async-start(bf16[4,128,256]{2,1,0:T(8,128)(2,1)} %shard_map.46), calls=%async_computation | async-start | bytes 524288 | tf_op jit(solution)/shard_map/all_to_all | solution.py:136
  7.0 13.4 %copy-start.5 = (bf16[2048]{0:T(1024)(128)(2,1)S(1)}, bf16[2048]{0:T(1024)(128)(2,1)}, u32[]{:S(2)}) copy-start(bf16[2048]{0:T(1024)(128)(2,1)} %gain_ref.1) | copy-start | bytes 12292
  21.2 1.0 copy-start.1
  22.2 38.0 %all-to-all-start.1 = ((bf16[8,128,512]{2,1,0:T(8,128)(2,1)}), bf16[8,128,512]{2,1,0:T(8,128)(2,1)S(1)}, u32[]{:S(2)}, u32[]{:S(2)}) async-start(bf16[8,128,512]{2,1,0:T(8,128)(2,1)} %copy-done.1), calls=%async_computation.1 | async-start | bytes 2097152 | tf_op jit(solution)/shard_map/all_to_all | solution.py:136
  28.5 63.0 %collective-permute-start = (bf16[256,2048]{1,0:T(8,128)(2,1)}, bf16[256,2048]{1,0:T(8,128)(2,1)S(1)}, u32[]{:S(2)}, u32[]{:S(2)}) collective-permute-start(bf16[256,2048]{1,0:T(8,128)(2,1)} %w_ref.1), channel_id=1, source_target_pairs={{0,1},{1,0},{2,3},{3,2},{4,5},{5,4},{6,7},{7,6},{8,9},{9,8},{10,11... | collective-permute-start | bytes 3145736 | tf_op jit(solution)/shard_map/ppermute | solution.py:148
  31.1 60.4 %copy-start = (bf16[256,2048]{1,0:T(8,128)(2,1)S(1)}, bf16[256,2048]{1,0:T(8,128)(2,1)}, u32[]{:S(2)}) copy-start(bf16[256,2048]{1,0:T(8,128)(2,1)} %w_ref.1) | copy-start | bytes 3145732
  60.2 1.0 %copy-start.2 = (bf16[1024,256]{1,0:T(8,128)(2,1)S(1)}, bf16[1024,256]{1,0:T(8,128)(2,1)}, u32[]{:S(2)}) copy-start(bf16[1024,256]{1,0:T(8,128)(2,1)} %all-gather.1) | copy-start | bytes 1572868
  66.7 35.5 %copy-start.4 = (bf16[128,256]{1,0:T(8,128)(2,1)S(1)}, bf16[128,256]{1,0:T(8,128)(2,1)}, u32[]{:S(2)}) copy-start(bf16[128,256]{1,0:T(8,128)(2,1)} %tokens_ref.1) | copy-start | bytes 196612

commit v5 on v4

--- a/solution.py
+++ b/solution.py
@@ -67,29 +67,35 @@
         kv_ref[i, :, 256:] = turned
 
 
-def attend(q_ref, kv_ref, o_ref):
+def attend(q_ref, kv_ref, o_ref, parts, sent):
     factor = HEAD_DIM**-0.5 * LOG2E
+    copies = []
+    keys, values = [], []
     for h in range(2):
         cols = slice(h * HEAD_DIM, (h + 1) * HEAD_DIM)
         vcols = slice((2 + h) * HEAD_DIM, (3 + h) * HEAD_DIM)
-        keys = kv_ref[:, :, cols].reshape(2 * KEY_GROUP * ROWS, HEAD_DIM)
-        values = jnp.concatenate(
-            [
-                kv_ref[s, a * ROWS : (a + 1) * ROWS, vcols]
-                for s in range(KEY_GROUP)
-                for a in range(2)
-            ],
-            axis=1,
+        keys.append(kv_ref[:, :, cols].reshape(2 * KEY_GROUP * ROWS, HEAD_DIM))
+        values.append(
+            jnp.concatenate(
+                [
+                    kv_ref[s, a * ROWS : (a + 1) * ROWS, vcols]
+                    for s in range(KEY_GROUP)
+                    for a in range(2)
+                ],
+                axis=1,
+            )
         )
-        for pair in range(QUERY_GROUP // 2):
+    for pair in range(QUERY_GROUP // 2):
+        for h in range(2):
+            cols = slice(h * HEAD_DIM, (h + 1) * HEAD_DIM)
             query = q_ref[2 * pair : 2 * pair + 2, :, cols].reshape(2 * ROWS, HEAD_DIM)
             scores = lax.dot_general(
-                keys, query, (((1,), (1,)), ((), ())), preferred_element_type=f32
+                keys[h], query, (((1,), (1,)), ((), ())), preferred_element_type=f32
             )
             highest = jnp.max(scores, axis=0, keepdims=True)
             expon = jnp.exp2((scores - highest) * factor)
             denom = jnp.sum(expon, axis=0, keepdims=True)
-            context = jnp.dot(values, expon.astype(bf16), preferred_element_type=f32)
+            context = jnp.dot(values[h], expon.astype(bf16), preferred_element_type=f32)
             context = (context / denom).astype(bf16)
             level = highest * factor + jnp.log2(denom)
             first = level.astype(bf16).astype(f32)
@@ -100,8 +106,13 @@
             ).astype(bf16)
             for i in range(2):
                 span = slice(i * ROWS, (i + 1) * ROWS)
-                o_ref[2 * pair + i, :HEAD_DIM, cols] = context[:, span]
-                o_ref[2 * pair + i, HEAD_DIM:, cols] = stats[:, span]
+                parts[2 * pair + i, :HEAD_DIM, cols] = context[:, span]
+                parts[2 * pair + i, HEAD_DIM:, cols] = stats[:, span]
+        blocks = pl.ds(2 * pair, 2)
+        copies.append(pltpu.make_async_copy(parts.at[blocks], o_ref.at[blocks], sent.at[pair]))
+        copies[-1].start()
+    for copy in copies:
+        copy.wait()
 
 
 def combine(o_ref, c_ref):
@@ -163,7 +174,11 @@
         attend,
         out_shape=shape((QUERY_GROUP, HEAD_DIM + STAT_ROWS, 2 * ROWS), bf16),
         in_specs=vmem(2),
-        out_specs=vmem(1)[0],
+        out_specs=pl.BlockSpec(memory_space=pl.ANY),
+        scratch_shapes=[
+            pltpu.VMEM((QUERY_GROUP, HEAD_DIM + STAT_ROWS, 2 * ROWS), bf16),
+            pltpu.SemaphoreType.DMA((QUERY_GROUP // 2,)),
+        ],
         compiler_params=limit(24),
         cost_estimate=pl.CostEstimate(
             flops=4 * 1024 * 1024 * 256, bytes_accessed=3 << 20, transcendentals=2 << 20

time: 105 us -> 106 us (level)
  Pallas kernels: 7.52 us -> 8.71 us
    pallas_call x1, Pallas kernels: 5.47 us -> 6.66 us  [on_device(): pl.pallas_call(attend, out_shape=shape((QUERY_GROUP, HEAD_DIM + STAT_ROWS...]
  transfers between devices with their start and end apart: 3 -> 3, of which waited for: 1 -> 1; matrix products, arithmetic and copies ran while one was open for 2% -> 2% of each run, Pallas kernels for 5% -> 7%
where the time goes in v5:
time: 106 us; the launch traced here: 104 us
  blocking collectives  71.7 us (68%)
  starting transfers between devices  14.3 us (13%)
  Pallas kernels  8.71 us (8%)
  local copies, waits for them, and re-layouts  4.94 us (5%)
  waiting for transfers between devices  3.56 us (3%)
    all_gather x1, blocking collectives, on_device(): q_here = lax.all_gather(q_blocks, 'z', axis=0)  29 us
    all_to_all x2, blocking collectives, exchange(): return lax.all_to_all(blocks, axes, 0, 0, tiled=True)  26.6 us
    all_to_all x2, starting transfers between devices, exchange(): return lax.all_to_all(blocks, axes, 0, 0, tiled=True)  11.8 us
    all_gather x1, blocking collectives, on_device(): lax.all_gather(context, 'core', axis=0)  8.31 us
    all_gather x1, blocking collectives, on_device(): whole = lax.all_gather(across, 'core', axis=0)  7.75 us
    pallas_call x1, Pallas kernels, on_device(): pl.pallas_call(attend, out_shape=shape((QUERY_GROUP, HEAD_DIM + STAT_ROWS...  6.66 us
    all_to_all x2, waiting for transfers between devices, exchange(): return lax.all_to_all(blocks, axes, 0, 0, tiled=True)  3.55 us
    unnamed x12, local copies, waits for them, and re-layouts  2.87 us
  transfers between devices with their start and end apart: 3, of which 1 were waited for; matrix products, arithmetic and copies ran while one was open for 2% of the time, Pallas kernels for 7%

profile of v5, /device:TPU:1, one launch (start us, length us, event | category | flops | bytes accessed | tf_op | source)
XLA Modules:
  0.0 104.0 jit_solution(3080210385980510830)
XLA Ops:
  0.0 0.8 copy-done.3
  0.8 0.7 shard_map.46
  1.6 5.4 %all-to-all-start = ((bf16[4,128,256]{2,1,0:T(8,128)(2,1)}), bf16[4,128,256]{2,1,0:T(8,128)(2,1)S(1)}, u32[]{:S(2)}, u32[]{:S(2)}) async-start(bf16[4,128,256]{2,1,0:T(8,128)(2,1)} %shard_map.46), calls=%async_computation | async-start | bytes 524288 | tf_op jit(solution)/shard_map/all_to_all | solution.py:147
  7.0 2.1 %slice_bitcast_fusion = (bf16[2048,256]{1,0:T(8,128)(2,1)S(1)}, bf16[2048,256]{1,0:T(8,128)(2,1)S(1)}, bf16[2048,256]{1,0:T(8,128)(2,1)S(1)}) fusion(bf16[3,2048,256]{2,1,0:T(8,128)(2,1)} %param.6), kind=kLoop, calls=%fused_computation | loop fusion | bytes 6291456 | tf_op jit(solution)/shard_map/squeeze | solution.py:170
  9.1 3.5 %all-to-all-done = bf16[4,128,256]{2,1,0:T(8,128)(2,1)S(1)} async-done(((bf16[4,128,256]{2,1,0:T(8,128)(2,1)}), bf16[4,128,256]{2,1,0:T(8,128)(2,1)S(1)}, u32[]{:S(2)}, u32[]{:S(2)}) %all-to-all-start) | async-done | bytes 262176 | tf_op jit(solution)/shard_map/all_to_all | solution.py:147
  12.6 7.8 %all-gather = bf16[8,128,256]{2,1,0:T(8,128)(2,1)S(1)} all-gather(bf16[4,128,256]{2,1,0:T(8,128)(2,1)S(1)} %all-to-all-done), channel_id=2, replica_groups=mesh['z'=8,'y_hi'=2,'x'=4,'y_lo'=4,'core'=2] {'core'}, dimensions={0}, use_global_device_ids=true | all-gather | bytes 786432 | tf_op jit(solution)/shard_map/all_gather | solution.py:160
  20.4 0.8 shard_map.47
  21.2 0.0 copy-start.1
  21.2 1.0 copy-done.1
  22.2 6.4 %all-to-all-start.1 = ((bf16[8,128,512]{2,1,0:T(8,128)(2,1)}), bf16[8,128,512]{2,1,0:T(8,128)(2,1)S(1)}, u32[]{:S(2)}, u32[]{:S(2)}) async-start(bf16[8,128,512]{2,1,0:T(8,128)(2,1)} %copy-done.1), calls=%async_computation.1 | async-start | bytes 2097152 | tf_op jit(solution)/shard_map/all_to_all | solution.py:147
  28.5 2.6 %collective-permute-start = (bf16[256,2048]{1,0:T(8,128)(2,1)}, bf16[256,2048]{1,0:T(8,128)(2,1)S(1)}, u32[]{:S(2)}, u32[]{:S(2)}) collective-permute-start(bf16[256,2048]{1,0:T(8,128)(2,1)} %w_ref.1), channel_id=1, source_target_pairs={{0,1},{1,0},{2,3},{3,2},{4,5},{5,4},{6,7},{7,6},{8,9},{9,8},{10,11... | collective-permute-start | bytes 3145736 | tf_op jit(solution)/shard_map/ppermute | solution.py:159
  31.1 0.0 copy-start
  31.1 29.0 %all-gather.1 = bf16[1024,256]{1,0:T(8,128)(2,1)} all-gather(bf16[128,256]{1,0:T(8,128)(2,1)S(1)} %get-tuple-element.7), channel_id=3, replica_groups=mesh['z'=8,'y_hi'=2,'x'=4,'y_lo'=4,'core'=2] {'z'}, dimensions={0}, use_global_device_ids=true | all-gather | bytes 589824 | tf_op jit(solution)/shard_map/all_gather | solution.py:172
  60.2 0.0 all-to-all-done.1
  60.2 1.0 %copy-done.2 = bf16[1024,256]{1,0:T(8,128)(2,1)S(1)} copy-done((bf16[1024,256]{1,0:T(8,128)(2,1)S(1)}, bf16[1024,256]{1,0:T(8,128)(2,1)}, u32[]{:S(2)}) %copy-start.2) | copy-done | bytes 524312
  61.2 6.7 %shard_map.48 = bf16[8,136,256]{2,1,0:T(8,128)(2,1)S(1)} custom-call(bf16[8,128,256]{2,1,0:T(8,128)(2,1)S(1)} %bitcast.13, bf16[4,256,512]{2,1,0:T(8,128)(2,1)S(1)} %bitcast.11), custom_call_target="tpu_custom_call" | custom-call | flops 1073741824 | bytes 3145728 | tf_op jit(solution)/shard_map/pallas_call | solution.py:173
  67.9 0.0 copy-start.4
  67.9 16.4 %all_to_all.20.o_ref = bf16[8,136,256]{2,1,0:T(8,128)(2,1)S(1)} all-to-all(bf16[8,136,256]{2,1,0:T(8,128)(2,1)S(1)} %shard_map.48), channel_id=1, replica_groups=mesh['z'=8,'y_hi'=2,'x'=4,'y_lo'=4,'core'=2] {'z'}, dimensions={0} | all-to-all | bytes 1114112 | tf_op jit(solution)/shard_map/all_to_all | solution.py:147
  84.2 0.1 shard_map.49
  84.4 8.3 %all-gather.2 = bf16[256,256]{1,0:T(8,128)(2,1)S(1)} all-gather(bf16[128,256]{1,0:T(8,128)(2,1)S(1)} %shard_map.49), channel_id=4, replica_groups=mesh['z'=8,'y_hi'=2,'x'=4,'y_lo'=4,'core'=2] {'core'}, dimensions={0}, use_global_device_ids=true | all-gather | bytes 196608 | tf_op jit(solution)/shard_map/all_gather | solution.py:201
  92.7 0.0 collective-permute-done.w_other_ref
  92.7 0.3 shard_map.50
  93.1 10.3 %all_to_all.21 = bf16[4,128,256]{2,1,0:T(8,128)(2,1)S(1)} all-to-all(bf16[4,128,256]{2,1,0:T(8,128)(2,1)S(1)} %shard_map.50), channel_id=1, replica_groups=mesh['z'=8,'y_hi'=2,'x'=4,'y_lo'=4,'core'=2] {'y_lo'}, dimensions={0} | all-to-all | bytes 524288 | tf_op jit(solution)/shard_map/all_to_all | solution.py:147
  103.4 0.6 add_convert_fusion
  (7 shorter events, 0.0 us)
Async XLA Ops:
  0.0 0.8 copy-start.3
  1.6 11.0 %all-to-all-start = ((bf16[4,128,256]{2,1,0:T(8,128)(2,1)}), bf16[4,128,256]{2,1,0:T(8,128)(2,1)S(1)}, u32[]{:S(2)}, u32[]{:S(2)}) async-start(bf16[4,128,256]{2,1,0:T(8,128)(2,1)} %shard_map.46), calls=%async_computation | async-start | bytes 524288 | tf_op jit(solution)/shard_map/all_to_all | solution.py:147
  7.0 13.4 %copy-start.5 = (bf16[2048]{0:T(1024)(128)(2,1)S(1)}, bf16[2048]{0:T(1024)(128)(2,1)}, u32[]{:S(2)}) copy-start(bf16[2048]{0:T(1024)(128)(2,1)} %gain_ref.1) | copy-start | bytes 12292
  21.2 1.0 copy-start.1
  22.2 38.0 %all-to-all-start.1 = ((bf16[8,128,512]{2,1,0:T(8,128)(2,1)}), bf16[8,128,512]{2,1,0:T(8,128)(2,1)S(1)}, u32[]{:S(2)}, u32[]{:S(2)}) async-start(bf16[8,128,512]{2,1,0:T(8,128)(2,1)} %copy-done.1), calls=%async_computation.1 | async-start | bytes 2097152 | tf_op jit(solution)/shard_map/all_to_all | solution.py:147
  28.5 64.2 %collective-permute-start = (bf16[256,2048]{1,0:T(8,128)(2,1)}, bf16[256,2048]{1,0:T(8,128)(2,1)S(1)}, u32[]{:S(2)}, u32[]{:S(2)}) collective-permute-start(bf16[256,2048]{1,0:T(8,128)(2,1)} %w_ref.1), channel_id=1, source_target_pairs={{0,1},{1,0},{2,3},{3,2},{4,5},{5,4},{6,7},{7,6},{8,9},{9,8},{10,11... | collective-permute-start | bytes 3145736 | tf_op jit(solution)/shard_map/ppermute | solution.py:159
  31.1 61.6 %copy-start = (bf16[256,2048]{1,0:T(8,128)(2,1)S(1)}, bf16[256,2048]{1,0:T(8,128)(2,1)}, u32[]{:S(2)}) copy-start(bf16[256,2048]{1,0:T(8,128)(2,1)} %w_ref.1) | copy-start | bytes 3145732
  60.2 1.0 %copy-start.2 = (bf16[1024,256]{1,0:T(8,128)(2,1)S(1)}, bf16[1024,256]{1,0:T(8,128)(2,1)}, u32[]{:S(2)}) copy-start(bf16[1024,256]{1,0:T(8,128)(2,1)} %all-gather.1) | copy-start | bytes 1572868
  67.9 35.5 %copy-start.4 = (bf16[128,256]{1,0:T(8,128)(2,1)S(1)}, bf16[128,256]{1,0:T(8,128)(2,1)}, u32[]{:S(2)}) copy-start(bf16[128,256]{1,0:T(8,128)(2,1)} %tokens_ref.1) | copy-start | bytes 196612

commit v6 on v5

--- a/solution.py
+++ b/solution.py
@@ -143,6 +143,13 @@
         out_ref[y] = jnp.dot(turned, weights, preferred_element_type=f32).astype(bf16)
 
 
+def finish(tokens_ref, parts_ref, out_ref):
+    total = parts_ref[0].astype(f32)
+    for y in range(1, 4):
+        total += parts_ref[y].astype(f32)
+    out_ref[...] = (tokens_ref[...].astype(f32) + total).astype(bf16)
+
+
 def exchange(blocks, axes):
     return lax.all_to_all(blocks, axes, 0, 0, tiled=True)
 
@@ -199,8 +206,13 @@
         out_specs=vmem(1)[0],
         compiler_params=limit(16),
     )(lax.all_gather(context, "core", axis=0), w_out, w_other)
-    summed = jnp.sum(exchange(projected, "y_lo").astype(f32), axis=0)
-    return (tokens.astype(f32) + summed).astype(bf16)
+    return pl.pallas_call(
+        finish,
+        out_shape=shape(tokens.shape, bf16),
+        in_specs=vmem(2),
+        out_specs=vmem(1)[0],
+        compiler_params=limit(4),
+    )(tokens, exchange(projected, "y_lo"))
 
 
 def solution(mesh):

time: 106 us -> 106 us (level)
  no operation moved by 1% of the time
where the time goes in v6:
time: 106 us; the launch traced here: 104 us
  blocking collectives  71.7 us (68%)
  starting transfers between devices  14.3 us (13%)
  Pallas kernels  9.38 us (9%)
  local copies, waits for them, and re-layouts  4.94 us (5%)
  waiting for transfers between devices  3.56 us (3%)
    all_gather x1, blocking collectives, on_device(): q_here = lax.all_gather(q_blocks, 'z', axis=0)  29.1 us
    all_to_all x2, blocking collectives, exchange(): return lax.all_to_all(blocks, axes, 0, 0, tiled=True)  26.6 us
    all_to_all x2, starting transfers between devices, exchange(): return lax.all_to_all(blocks, axes, 0, 0, tiled=True)  11.8 us
    all_gather x1, blocking collectives, on_device(): lax.all_gather(context, 'core', axis=0)  8.33 us
    all_gather x1, blocking collectives, on_device(): whole = lax.all_gather(across, 'core', axis=0)  7.75 us
    pallas_call x1, Pallas kernels, on_device(): pl.pallas_call(attend, out_shape=shape((QUERY_GROUP, HEAD_DIM + STAT_ROWS...  6.66 us
    all_to_all x2, waiting for transfers between devices, exchange(): return lax.all_to_all(blocks, axes, 0, 0, tiled=True)  3.55 us
    unnamed x12, local copies, waits for them, and re-layouts  2.87 us
  transfers between devices with their start and end apart: 3, of which 1 were waited for; matrix products, arithmetic and copies ran while one was open for 2% of the time, Pallas kernels for 7%

profile of v6, /device:TPU:1, one launch (start us, length us, event | category | flops | bytes accessed | tf_op | source)
XLA Modules:
  0.0 104.0 jit_solution(14194345237913355577)
XLA Ops:
  0.0 0.8 copy-done.3
  0.8 0.7 shard_map.46
  1.6 5.4 %all-to-all-start = ((bf16[4,128,256]{2,1,0:T(8,128)(2,1)}), bf16[4,128,256]{2,1,0:T(8,128)(2,1)S(1)}, u32[]{:S(2)}, u32[]{:S(2)}) async-start(bf16[4,128,256]{2,1,0:T(8,128)(2,1)} %shard_map.46), calls=%async_computation | async-start | bytes 524288 | tf_op jit(solution)/shard_map/all_to_all | solution.py:154
  7.0 2.1 %slice_bitcast_fusion = (bf16[2048,256]{1,0:T(8,128)(2,1)S(1)}, bf16[2048,256]{1,0:T(8,128)(2,1)S(1)}, bf16[2048,256]{1,0:T(8,128)(2,1)S(1)}) fusion(bf16[3,2048,256]{2,1,0:T(8,128)(2,1)} %param.6), kind=kLoop, calls=%fused_computation | loop fusion | bytes 6291456 | tf_op jit(solution)/shard_map/squeeze | solution.py:177
  9.0 3.5 %all-to-all-done = bf16[4,128,256]{2,1,0:T(8,128)(2,1)S(1)} async-done(((bf16[4,128,256]{2,1,0:T(8,128)(2,1)}), bf16[4,128,256]{2,1,0:T(8,128)(2,1)S(1)}, u32[]{:S(2)}, u32[]{:S(2)}) %all-to-all-start) | async-done | bytes 262176 | tf_op jit(solution)/shard_map/all_to_all | solution.py:154
  12.6 7.8 %all-gather = bf16[8,128,256]{2,1,0:T(8,128)(2,1)S(1)} all-gather(bf16[4,128,256]{2,1,0:T(8,128)(2,1)S(1)} %all-to-all-done), channel_id=2, replica_groups=mesh['z'=8,'y_hi'=2,'x'=4,'y_lo'=4,'core'=2] {'core'}, dimensions={0}, use_global_device_ids=true | all-gather | bytes 786432 | tf_op jit(solution)/shard_map/all_gather | solution.py:167
  20.4 0.8 shard_map.47
  21.2 0.0 copy-start.1
  21.2 1.0 copy-done.1
  22.2 6.4 %all-to-all-start.1 = ((bf16[8,128,512]{2,1,0:T(8,128)(2,1)}), bf16[8,128,512]{2,1,0:T(8,128)(2,1)S(1)}, u32[]{:S(2)}, u32[]{:S(2)}) async-start(bf16[8,128,512]{2,1,0:T(8,128)(2,1)} %copy-done.1), calls=%async_computation.1 | async-start | bytes 2097152 | tf_op jit(solution)/shard_map/all_to_all | solution.py:154
  28.5 2.5 %collective-permute-start = (bf16[256,2048]{1,0:T(8,128)(2,1)}, bf16[256,2048]{1,0:T(8,128)(2,1)S(1)}, u32[]{:S(2)}, u32[]{:S(2)}) collective-permute-start(bf16[256,2048]{1,0:T(8,128)(2,1)} %w_ref.1), channel_id=1, source_target_pairs={{0,1},{1,0},{2,3},{3,2},{4,5},{5,4},{6,7},{7,6},{8,9},{9,8},{10,11... | collective-permute-start | bytes 3145736 | tf_op jit(solution)/shard_map/ppermute | solution.py:166
  31.1 0.0 copy-start
  31.1 29.1 %all-gather.1 = bf16[1024,256]{1,0:T(8,128)(2,1)} all-gather(bf16[128,256]{1,0:T(8,128)(2,1)S(1)} %get-tuple-element.7), channel_id=3, replica_groups=mesh['z'=8,'y_hi'=2,'x'=4,'y_lo'=4,'core'=2] {'z'}, dimensions={0}, use_global_device_ids=true | all-gather | bytes 589824 | tf_op jit(solution)/shard_map/all_gather | solution.py:179
  60.2 0.0 all-to-all-done.1
  60.2 1.0 %copy-done.2 = bf16[1024,256]{1,0:T(8,128)(2,1)S(1)} copy-done((bf16[1024,256]{1,0:T(8,128)(2,1)S(1)}, bf16[1024,256]{1,0:T(8,128)(2,1)}, u32[]{:S(2)}) %copy-start.2) | copy-done | bytes 524312
  61.2 6.7 %shard_map.48 = bf16[8,136,256]{2,1,0:T(8,128)(2,1)S(1)} custom-call(bf16[8,128,256]{2,1,0:T(8,128)(2,1)S(1)} %bitcast.13, bf16[4,256,512]{2,1,0:T(8,128)(2,1)S(1)} %bitcast.11), custom_call_target="tpu_custom_call" | custom-call | flops 1073741824 | bytes 3145728 | tf_op jit(solution)/shard_map/pallas_call | solution.py:180
  67.9 0.0 copy-start.4
  67.9 16.3 %all_to_all.20.o_ref = bf16[8,136,256]{2,1,0:T(8,128)(2,1)S(1)} all-to-all(bf16[8,136,256]{2,1,0:T(8,128)(2,1)S(1)} %shard_map.48), channel_id=1, replica_groups=mesh['z'=8,'y_hi'=2,'x'=4,'y_lo'=4,'core'=2] {'z'}, dimensions={0} | all-to-all | bytes 1114112 | tf_op jit(solution)/shard_map/all_to_all | solution.py:154
  84.2 0.1 shard_map.49
  84.4 8.3 %all-gather.2 = bf16[256,256]{1,0:T(8,128)(2,1)S(1)} all-gather(bf16[128,256]{1,0:T(8,128)(2,1)S(1)} %shard_map.49), channel_id=4, replica_groups=mesh['z'=8,'y_hi'=2,'x'=4,'y_lo'=4,'core'=2] {'core'}, dimensions={0}, use_global_device_ids=true | all-gather | bytes 196608 | tf_op jit(solution)/shard_map/all_gather | solution.py:208
  92.7 0.0 collective-permute-done.w_other_ref
  92.7 0.3 shard_map.50
  93.0 10.3 %all_to_all.21.parts_ref = bf16[4,128,256]{2,1,0:T(8,128)(2,1)S(1)} all-to-all(bf16[4,128,256]{2,1,0:T(8,128)(2,1)S(1)} %shard_map.50), channel_id=1, replica_groups=mesh['z'=8,'y_hi'=2,'x'=4,'y_lo'=4,'core'=2] {'y_lo'}, dimensions={0} | all-to-all | bytes 524288 | tf_op jit(solution)/shard_map/all_to_all | solution.py:154
  103.3 0.7 shard_map.51
  (6 shorter events, 0.0 us)
Async XLA Ops:
  0.0 0.8 copy-start.3
  1.6 11.0 %all-to-all-start = ((bf16[4,128,256]{2,1,0:T(8,128)(2,1)}), bf16[4,128,256]{2,1,0:T(8,128)(2,1)S(1)}, u32[]{:S(2)}, u32[]{:S(2)}) async-start(bf16[4,128,256]{2,1,0:T(8,128)(2,1)} %shard_map.46), calls=%async_computation | async-start | bytes 524288 | tf_op jit(solution)/shard_map/all_to_all | solution.py:154
  7.0 13.4 %copy-start.5 = (bf16[2048]{0:T(1024)(128)(2,1)S(1)}, bf16[2048]{0:T(1024)(128)(2,1)}, u32[]{:S(2)}) copy-start(bf16[2048]{0:T(1024)(128)(2,1)} %gain_ref.1) | copy-start | bytes 12292
  21.2 1.0 copy-start.1
  22.2 38.0 %all-to-all-start.1 = ((bf16[8,128,512]{2,1,0:T(8,128)(2,1)}), bf16[8,128,512]{2,1,0:T(8,128)(2,1)S(1)}, u32[]{:S(2)}, u32[]{:S(2)}) async-start(bf16[8,128,512]{2,1,0:T(8,128)(2,1)} %copy-done.1), calls=%async_computation.1 | async-start | bytes 2097152 | tf_op jit(solution)/shard_map/all_to_all | solution.py:154
  28.5 64.2 %collective-permute-start = (bf16[256,2048]{1,0:T(8,128)(2,1)}, bf16[256,2048]{1,0:T(8,128)(2,1)S(1)}, u32[]{:S(2)}, u32[]{:S(2)}) collective-permute-start(bf16[256,2048]{1,0:T(8,128)(2,1)} %w_ref.1), channel_id=1, source_target_pairs={{0,1},{1,0},{2,3},{3,2},{4,5},{5,4},{6,7},{7,6},{8,9},{9,8},{10,11... | collective-permute-start | bytes 3145736 | tf_op jit(solution)/shard_map/ppermute | solution.py:166
  31.1 61.6 %copy-start = (bf16[256,2048]{1,0:T(8,128)(2,1)S(1)}, bf16[256,2048]{1,0:T(8,128)(2,1)}, u32[]{:S(2)}) copy-start(bf16[256,2048]{1,0:T(8,128)(2,1)} %w_ref.1) | copy-start | bytes 3145732
  60.2 1.0 %copy-start.2 = (bf16[1024,256]{1,0:T(8,128)(2,1)S(1)}, bf16[1024,256]{1,0:T(8,128)(2,1)}, u32[]{:S(2)}) copy-start(bf16[1024,256]{1,0:T(8,128)(2,1)} %all-gather.1) | copy-start | bytes 1572868
  67.9 35.4 %copy-start.4 = (bf16[128,256]{1,0:T(8,128)(2,1)S(1)}, bf16[128,256]{1,0:T(8,128)(2,1)}, u32[]{:S(2)}) copy-start(bf16[128,256]{1,0:T(8,128)(2,1)} %tokens_ref.3) | copy-start | bytes 196612
